TPU v7x, 16 devices: a whole 2x2x2 slice. The times are simulated.
16 devices in a mesh: rep: 1, dp: 16 (over x, y, z, core).
Axes of the slice: x: 2, y: 2, z: 2, core: 2. Of those that a mesh axis runs over, the one named last changes fastest.
Arguments:
- x: bfloat16 [16, 2048, 768], P(('rep', 'dp'))
- dy: bfloat16 [16, 2048, 768], P(('rep', 'dp'))
- w_gate: bfloat16 [2, 768, 6144], replicated
- w_up: bfloat16 [2, 768, 6144], replicated
- w_down: bfloat16 [2, 6144, 768], replicated
- m_w_gate: float32 [2, 768, 6144], replicated
- m_w_up: float32 [2, 768, 6144], replicated
- m_w_down: float32 [2, 6144, 768], replicated
- v_w_gate: float32 [2, 768, 6144], replicated
- v_w_up: float32 [2, 768, 6144], replicated
- v_w_down: float32 [2, 6144, 768], replicated
Outputs:
- output 1: bfloat16 [2, 768, 6144], P('rep')
- output 2: bfloat16 [2, 768, 6144], P('rep')
- output 3: bfloat16 [2, 6144, 768], P('rep')
- output 4: float32 [2, 768, 6144], P('rep')
- output 5: float32 [2, 768, 6144], P('rep')
- output 6: float32 [2, 6144, 768], P('rep')
- output 7: float32 [2, 768, 6144], P('rep')
- output 8: float32 [2, 768, 6144], P('rep')
- output 9: float32 [2, 6144, 768], P('rep')
All inputs are finite; a program needn't handle non-finite values.
Results may differ from a plain program's by a relative error of at most 0.022.
Values are sent between devices in bfloat16 or wider.
A program may use at most 3 GiB of HBM per device.

v0:
```python
import jax
import jax.numpy as jnp
from jax import lax
from jax.sharding import PartitionSpec as P

NAMES = ("w_gate", "w_up", "w_down")


def matmul(a, w):
    return jnp.dot(a, w, preferred_element_type=jnp.float32).astype(jnp.bfloat16)


def normed(h):
    wide = h.astype(jnp.float32)
    scale = lax.rsqrt(jnp.mean(wide**2, -1, keepdims=True) + 1e-6)
    return (wide * scale).astype(jnp.bfloat16)


def layer(h, w):
    a = normed(h)
    gate = jnp.dot(a, w["w_gate"], preferred_element_type=jnp.float32)
    up = jnp.dot(a, w["w_up"], preferred_element_type=jnp.float32)
    return h + matmul((jax.nn.silu(gate) * up).astype(jnp.bfloat16), w["w_down"])


def adamw(w, m, v, g):
    m = 0.9 * m + 0.1 * g
    v = 0.95 * v + 0.05 * g * g
    step = m * lax.rsqrt(v + 1e-8) + 0.1 * w
    return (w - 0.02 * step).astype(jnp.bfloat16), m, v


def solution(mesh):
    def step(x, dy, *arrays):
        weights, m, v = (arrays[i : i + 3] for i in (0, 3, 6))
        layers = weights[0].shape[0]
        h, kept = x[0], []
        for number in range(layers):
            kept.append(h)
            h = layer(h, {name: w[number] for name, w in zip(NAMES, weights, strict=True)})
        by_h, summed = dy[0], [None] * layers
        for number in reversed(range(layers)):
            _, back = jax.vjp(lambda w, h: layer(h, w), {name: w[number] for name, w in zip(NAMES, weights, strict=True)}, kept[number])
            by_w, by_h = back(by_h)
            summed[number] = [lax.psum(by_w[name], "dp") for name in NAMES]
        gradients = [jnp.stack([summed[number][i] for number in range(layers)]).astype(jnp.float32) for i in range(3)]
        new = [adamw(w.astype(jnp.float32), m, v, g) for w, m, v, g in zip(weights, m, v, gradients, strict=True)]
        return tuple(one[which] for which in range(3) for one in new)

    return jax.shard_map(
        step,
        mesh=mesh,
        in_specs=(P(("rep", "dp"), None, None),) * 2 + (P(None, None, None),) * 9,
        out_specs=(P("rep", None, None),) * 9,
        check_vma=False,
    )
```

profile of v0, /device:TPU:0, one launch (start us, length us, event | category | flops | bytes accessed | tf_op | source)
XLA Modules:
  0.0 1253.9 jit_solution(11256292554397344135)
XLA Ops:
  7.2 0.0 all-reduce.3.cloned.1.call-start
  7.2 3.2 copy.20
  10.4 0.0 copy-start
  10.4 0.7 fusion.69
  11.1 5.1 copy.21
  16.2 26.6 %convolution_convert_fusion.1 = bf16[2048,6144]{1,0:T(8,128)(2,1)} fusion(bf16[2,6144,768]{2,1,0:T(8,128)(2,1)} %param.15, bf16[1,2048,768]{2,1,0:T(8,128)(2,1)} %param.12), kind=kOutput, calls=%fused_computation.52 | convolution fusion | flops 19339935744 | bytes 37748736 | tf_op jit(solution)/shard_map/transpose(jvp())/dot_general | solution.py:10
  42.9 0.0 copy-done
  42.9 0.0 copy-done.4
  42.9 28.9 %fusion.49 = f32[2048,6144]{1,0:T(8,128)} fusion(bf16[2,768,6144]{2,1,0:T(8,128)(2,1)} %param.13, bf16[1,2048,768]{2,1,0:T(8,128)(2,1)S(1)} %copy-done.4, f32[2048]{0:T(1024)S(1)} %add_rsqrt_fusion), kind=kOutput, calls=%fused_computation.79 | convolution fusion | flops 19332071424 | bytes 62922752 | tf_op jit(solution)/shard_map/dot_general | solution.py:21
  71.8 0.0 copy-done.11
  71.8 49.3 %multiply_convert_fusion.1 = (bf16[2048,6144]{1,0:T(8,128)(2,1)}, f32[2048,6144]{1,0:T(8,128)}) fusion(f32[2048,6144]{1,0:T(8,128)} %fusion.49, bf16[2,768,6144]{2,1,0:T(8,128)(2,1)} %param.14, bf16[1,2048,768]{2,1,0:T(8,128)(2,1)} %param.11, f32[2048]{0:T(1024)S(1)} %add_rsqrt_fusion), kind=kOutput, calls=%fused_computation.20 | convolution fusion | flops 19407568896 | bytes 138420224 | tf_op jit(solution)/shard_map/dot_general | solution.py:22
  121.0 0.0 copy-done.1
  121.1 26.9 %fusion.73 = (f32[2048]{0:T(1024)S(1)}, bf16[2048,768]{0,1:T(8,128)(2,1)}) fusion(bf16[2048,6144]{1,0:T(8,128)(2,1)} %get-tuple-element.24, bf16[2,6144,768]{2,1,0:T(8,128)(2,1)} %param.15, bf16[1,2048,768]{1,2,0:T(8,128)(2,1)S(1)} %copy-done.1), kind=kOutput, calls=%fused_computation.103 | convolution fusion | flops 19335215104 | bytes 40902656 | tf_op jit(solution)/shard_map/dot_general | solution.py:10
  148.0 0.0 copy-start.6
  148.0 29.9 %fusion.36 = f32[2048,6144]{1,0:T(8,128)} fusion(bf16[2,768,6144]{2,1,0:T(8,128)(2,1)} %param.14, bf16[2048,768]{0,1:T(8,128)(2,1)} %get-tuple-element.27, f32[2048]{0:T(1024)S(1)} %fusion.102), kind=kOutput, calls=%fused_computation.66 | convolution fusion | flops 19332071424 | bytes 62922752 | tf_op jit(solution)/shard_map/jvp()/dot_general | solution.py:22
  177.9 64.0 %fusion.2 = (bf16[2048,6144]{1,0:T(8,128)(2,1)}, f32[2048,6144]{1,0:T(8,128)}) fusion(f32[2048,6144]{1,0:T(8,128)} %fusion.36, bf16[2048,6144]{1,0:T(8,128)(2,1)} %convolution_convert_fusion.1, bf16[2,768,6144]{2,1,0:T(8,128)(2,1)} %param.13, bf16[2048,768]{0,1:T(8,128)(2,1)S(1)} %copy-done.6, f32[2048]{0:T(1024)S(1)} %fusion.102), kind=kOutput, calls=%fused_computation.11 | convolution fusion | flops 19483066368 | bytes 163586048 | tf_op jit(solution)/shard_map/jvp()/dot_general | solution.py:21
  242.0 33.1 %fusion.76 = bf16[2048,768]{0,1:T(8,128)(2,1)} fusion(bf16[2,768,6144]{2,1,0:T(8,128)(2,1)} %param.14, bf16[2048,6144]{1,0:T(8,128)(2,1)} %convolution_convert_fusion.1, f32[2048,6144]{1,0:T(8,128)} %get-tuple-element.29), kind=kOutput, calls=%fused_computation.107 | convolution fusion | flops 19404423168 | bytes 88080384 | tf_op jit(solution)/shard_map/transpose(jvp())/dot_general | solution.py:22
  275.1 33.0 %fusion.56 = bf16[1,768,6144]{2,1,0:T(8,128)(2,1)} fusion(bf16[2048,6144]{1,0:T(8,128)(2,1)} %convolution_convert_fusion.1, bf16[2048,768]{0,1:T(8,128)(2,1)} %get-tuple-element.27, f32[2048]{0:T(1024)S(1)} %fusion.102, f32[2048,6144]{1,0:T(8,128)} %get-tuple-element.29), kind=kOutput, calls=%fused_computation.86 | convolution fusion | flops 19412287488 | bytes 88088576 | tf_op jit(solution)/shard_map/transpose(jvp())/dot_general | solution.py:22
  308.0 42.2 %fusion.61 = bf16[1,6144,768]{2,1,0:T(8,128)(2,1)} fusion(f32[2048,6144]{1,0:T(8,128)} %fusion.36, bf16[1,2048,768]{2,1,0:T(8,128)(2,1)S(1)} %copy-done.5, f32[2048,6144]{1,0:T(8,128)} %get-tuple-element.29), kind=kOutput, calls=%fused_computation.89 | convolution fusion | flops 19407568896 | bytes 113246208 | tf_op jit(solution)/shard_map/transpose(jvp())/dot_general | solution.py:10
  350.2 26.1 %fusion.57 = bf16[1,768,6144]{2,1,0:T(8,128)(2,1)} fusion(bf16[2048,6144]{1,0:T(8,128)(2,1)} %get-tuple-element.28, bf16[2048,768]{0,1:T(8,128)(2,1)} %get-tuple-element.27, f32[2048]{0:T(1024)S(1)} %fusion.102), kind=kOutput, calls=%fused_computation.87 | convolution fusion | flops 19332071424 | bytes 37756928 | tf_op jit(solution)/shard_map/transpose(jvp())/dot_general | solution.py:21
  376.3 27.7 %fusion.75 = (f32[2048]{0:T(1024)S(1)}, bf16[2048,768]{0,1:T(8,128)(2,1)}) fusion(bf16[2048,768]{0,1:T(8,128)(2,1)S(1)} %copy-done.7, bf16[2048,768]{0,1:T(8,128)(2,1)} %fusion.76, bf16[2048,6144]{1,0:T(8,128)(2,1)} %get-tuple-element.28, bf16[2,768,6144]{2,1,0:T(8,128)(2,1)} %param.13), kind=kOutput, calls=%fused_computation.105 | convolution fusion | flops 19335215104 | bytes 44048384 | tf_op jit(solution)/shard_map/transpose(jvp())/dot_general | solution.py:21
  404.0 5.8 fusion.86
  409.8 27.5 %convolution_convert_fusion = bf16[2048,6144]{1,0:T(8,128)(2,1)} fusion(bf16[2048,768]{0,1:T(8,128)(2,1)} %fusion.86, bf16[2,6144,768]{2,1,0:T(8,128)(2,1)} %param.15), kind=kOutput, calls=%fused_computation.51 | convolution fusion | flops 19339935744 | bytes 37748736 | tf_op jit(solution)/shard_map/transpose(jvp())/dot_general | solution.py:10
  437.4 0.0 copy-done.8
  437.4 26.9 %fusion.54 = bf16[1,6144,768]{2,1,0:T(8,128)(2,1)} fusion(bf16[2048,6144]{1,0:T(8,128)(2,1)} %get-tuple-element.24, bf16[2048,768]{0,1:T(8,128)(2,1)S(1)} %copy-done.8), kind=kOutput, calls=%fused_computation.84 | convolution fusion | flops 19332071424 | bytes 37748736 | tf_op jit(solution)/shard_map/transpose(jvp())/dot_general | solution.py:10
  464.3 0.0 copy-done.12
  464.3 32.3 %fusion.55 = bf16[1,768,6144]{2,1,0:T(8,128)(2,1)} fusion(bf16[2048,6144]{1,0:T(8,128)(2,1)} %convolution_convert_fusion, f32[2048,6144]{1,0:T(8,128)} %fusion.49, bf16[1,2048,768]{1,2,0:T(8,128)(2,1)S(1)} %copy-done.2, f32[2048]{0:T(1024)S(1)} %copy-done.12), kind=kOutput, calls=%fused_computation.85 | convolution fusion | flops 19412287488 | bytes 88088576 | tf_op jit(solution)/shard_map/transpose(jvp())/dot_general | solution.py:22
  496.6 47.0 %fusion.58 = bf16[1,768,6144]{2,1,0:T(8,128)(2,1)} fusion(f32[2048,6144]{1,0:T(8,128)} %fusion.49, f32[2048,6144]{1,0:T(8,128)} %get-tuple-element.25, bf16[2048,6144]{1,0:T(8,128)(2,1)} %convolution_convert_fusion, bf16[1,2048,768]{1,2,0:T(8,128)(2,1)S(1)} %copy-done.2, f32[2048]{0:T(1024)S(1)} %copy-done.12), kind=kOutput, calls=%fused_computation.88 | convolution fusion | flops 19475202048 | bytes 138420224 | tf_op jit(solution)/shard_map/transpose(jvp())/dot_general | solution.py:21
  543.6 0.0 all-reduce.3.cloned.1.call-update
  543.6 503.3 %all-reduce.3.cloned.1.call-done = (bf16[1,768,6144]{2,1,0:T(8,128)(2,1)}, bf16[1,768,6144]{2,1,0:T(8,128)(2,1)}, bf16[1,768,6144]{2,1,0:T(8,128)(2,1)}, bf16[1,...) async-done(((bf16[1,768,6144]{2,1,0:T(8,128)(2,1)}, bf16[1,768,6144]{2,1,0:T(8,128)(2,1)}, bf16[1,768,6144]{2,1,0:T(8,128)(2,1)}, ...) | async-done | bytes 56623120 | tf_op jit(solution)/shard_map/psum | solution.py:45
  1047.0 69.2 %fusion.21 = (bf16[2,6144,768]{2,1,0:T(8,128)(2,1)}, f32[2,6144,768]{2,1,0:T(8,128)}, f32[2,6144,768]{2,1,0:T(8,128)}) fusion(bf16[2,6144,768]{2,1,0:T(8,128)(2,1)} %param.15, bf16[1,6144,768]{2,1,0:T(8,128)(2,1)} %get-tuple-element.13, bf16[1,6144,768]{2,1,0:T(8,128)(2,1)} %get-tuple-element.14, f32[2,6144,768]{2,1,0:T(8,128)} %param.21, ...), kind=kLoop, calls=%fused_computation.42 | loop fusion | flops 179306496 | bytes 207618048 | tf_op jit(solution)/shard_map/convert_element_type | solution.py:30
  1116.2 130.3 %fusion.13 = (bf16[2,768,6144]{2,1,0:T(8,128)(2,1)}, f32[2,768,6144]{2,1,0:T(8,128)}, f32[2,768,6144]{2,1,0:T(8,128)}, bf16[2,768,6144]{2,1,0:T(8,128)(2,1)}, f3...) fusion(bf16[2,768,6144]{2,1,0:T(8,128)(2,1)} %param.13, bf16[1,768,6144]{2,1,0:T(8,128)(2,1)} %get-tuple-element.9, ...), kind=kLoop, calls=%fused_computation.34 | loop fusion | flops 358612992 | bytes 415236096 | tf_op jit(solution)/shard_map/convert_element_type | solution.py:30
  (21 shorter events, 0.1 us)
Async XLA Ops:
  7.2 1039.8 %all-reduce.3.cloned.1.call-start = ((), (), s32[]{:S(2)}) async-start(), calls=%async_computation | async-start | bytes 113246208 | tf_op jit(solution)/shard_map/psum | solution.py:45
  10.4 32.4 %copy-start = (bf16[1,2048,768]{1,2,0:T(8,128)(2,1)}, bf16[1,2048,768]{1,2,0:T(8,128)(2,1)S(1)}, u32[]{:S(2)}) copy-start(bf16[1,2048,768]{1,2,0:T(8,128)(2,1)S(1)} %copy.20) | copy-start | bytes 9437188
  11.1 60.7 %copy-start.11 = (f32[2048]{0:T(1024)}, f32[2048]{0:T(1024)S(1)}, u32[]{:S(2)}) copy-start(f32[2048]{0:T(1024)S(1)} %add_rsqrt_fusion) | copy-start | bytes 24580
  16.2 26.6 %copy-start.4 = (bf16[1,2048,768]{2,1,0:T(8,128)(2,1)S(1)}, bf16[1,2048,768]{2,1,0:T(8,128)(2,1)}, u32[]{:S(2)}) copy-start(bf16[1,2048,768]{2,1,0:T(8,128)(2,1)} %param.11) | copy-start | bytes 9437188
  71.8 49.3 %copy-start.1 = (bf16[1,2048,768]{1,2,0:T(8,128)(2,1)S(1)}, bf16[1,2048,768]{1,2,0:T(8,128)(2,1)}, u32[]{:S(2)}) copy-start(bf16[1,2048,768]{1,2,0:T(8,128)(2,1)} %copy-done) | copy-start | bytes 9437188
  148.0 29.9 %copy-start.9 = (f32[2048]{0:T(1024)}, f32[2048]{0:T(1024)S(1)}, u32[]{:S(2)}) copy-start(f32[2048]{0:T(1024)S(1)} %get-tuple-element.26) | copy-start | bytes 24580
  148.0 29.9 %copy-start.6 = (bf16[2048,768]{0,1:T(8,128)(2,1)S(1)}, bf16[2048,768]{0,1:T(8,128)(2,1)}, u32[]{:S(2)}) copy-start(bf16[2048,768]{0,1:T(8,128)(2,1)} %get-tuple-element.27) | copy-start | bytes 9437188
  275.1 33.0 %copy-start.5 = (bf16[1,2048,768]{2,1,0:T(8,128)(2,1)S(1)}, bf16[1,2048,768]{2,1,0:T(8,128)(2,1)}, u32[]{:S(2)}) copy-start(bf16[1,2048,768]{2,1,0:T(8,128)(2,1)} %param.12) | copy-start | bytes 9437188
  350.2 26.1 %copy-start.7 = (bf16[2048,768]{0,1:T(8,128)(2,1)S(1)}, bf16[2048,768]{0,1:T(8,128)(2,1)}, u32[]{:S(2)}) copy-start(bf16[2048,768]{0,1:T(8,128)(2,1)} %get-tuple-element.27) | copy-start | bytes 9437188
  376.3 27.7 %copy-start.10 = (f32[2048]{0:T(1024)S(1)}, f32[2048]{0:T(1024)}, u32[]{:S(2)}) copy-start(f32[2048]{0:T(1024)} %copy-done.9) | copy-start | bytes 24580
  376.3 27.7 %copy-start.3 = (bf16[1,2048,768]{1,2,0:T(8,128)(2,1)S(1)}, bf16[1,2048,768]{1,2,0:T(8,128)(2,1)}, u32[]{:S(2)}) copy-start(bf16[1,2048,768]{1,2,0:T(8,128)(2,1)} %copy.21) | copy-start | bytes 9437188
  409.8 27.5 %copy-start.8 = (bf16[2048,768]{0,1:T(8,128)(2,1)S(1)}, bf16[2048,768]{0,1:T(8,128)(2,1)}, u32[]{:S(2)}) copy-start(bf16[2048,768]{0,1:T(8,128)(2,1)} %fusion.86) | copy-start | bytes 9437188
  437.4 26.9 %copy-start.2 = (bf16[1,2048,768]{1,2,0:T(8,128)(2,1)S(1)}, bf16[1,2048,768]{1,2,0:T(8,128)(2,1)}, u32[]{:S(2)}) copy-start(bf16[1,2048,768]{1,2,0:T(8,128)(2,1)} %copy-done) | copy-start | bytes 9437188
  437.4 26.9 %copy-start.12 = (f32[2048]{0:T(1024)S(1)}, f32[2048]{0:T(1024)}, u32[]{:S(2)}) copy-start(f32[2048]{0:T(1024)} %copy-done.11) | copy-start | bytes 24580
Sparse Core Ops, SparseCore 0:
  543.8 503.1 all-reduce.2
where the time goes:
time: 1260 us; the launch traced here: 1250 us
  matrix products  521 us (41%)
  waiting for transfers between devices  503 us (40%)
  other arithmetic  206 us (16%)
  between operations  14.7 us (1%)
    psum x1, waiting for transfers between devices, step(): summed[number] = [lax.psum(by_w[name], 'dp') for name in NAMES]  503 us
    convert_element_type x2, other arithmetic, adamw(): return ((w - 0.02 * step).astype(jnp.bfloat16), m, v)  200 us
    dot_general x5, matrix products, layer(): gate = jnp.dot(a, w['w_gate'], preferred_element_type=jnp.float32)  194 us
    dot_general x5, matrix products, layer(): up = jnp.dot(a, w['w_up'], preferred_element_type=jnp.float32)  178 us
    dot_general x5, matrix products, matmul(): jnp.dot(a, w, preferred_element_type=jnp.float32).astype(jnp.bfloat16)  150 us
  transfers between devices with their start and end apart: 1, of which 1 were waited for; matrix products, arithmetic and copies ran while one was open for 0% of the time, Pallas kernels for 0%

commit v1 on v0

v1 whole, which is shorter than its diff:
```python
import functools

import jax
import jax.numpy as jnp
from jax import lax
from jax.experimental import pallas as pl
from jax.experimental.pallas import tpu as pltpu
from jax.sharding import PartitionSpec as P

BF, F32 = jnp.bfloat16, jnp.float32
T, D, FF = 2048, 768, 6144
BN = 512
VMEM_LIMIT = 60 * 1024 * 1024


def normed(h):
    wide = h.astype(F32)
    scale = lax.rsqrt(jnp.mean(wide**2, -1, keepdims=True) + 1e-6)
    return (wide * scale).astype(BF)


def sds(shape, dtype):
    return jax.ShapeDtypeStruct(shape, dtype)


def params(n=1):
    return pltpu.CompilerParams(dimension_semantics=("arbitrary",) * n, vmem_limit_bytes=VMEM_LIMIT)


def cost(matmuls, bytes_):
    return pl.CostEstimate(flops=int(2 * matmuls * T * D * FF), bytes_accessed=int(bytes_), transcendentals=0)


def mm(a, b, ca, cb):
    return lax.dot_general(a, b, (((ca,), (cb,)), ((), ())), preferred_element_type=F32)


def forward_kernel(rows, a_ref, g_ref, u_ref, act_ref):
    for r in range(0, T, rows):
        a = a_ref[r : r + rows, :]
        gate = mm(a, g_ref[0], 1, 0)
        up = mm(a, u_ref[0], 1, 0)
        act_ref[r : r + rows, :] = (gate * jax.nn.sigmoid(gate) * up).astype(BF)


def forward(a, w_gate, w_up, number):
    tile = lambda i: (number, 0, i)
    return pl.pallas_call(
        functools.partial(forward_kernel, 512),
        grid=(FF // BN,),
        in_specs=[
            pl.BlockSpec((T, D), lambda i: (0, 0)),
            pl.BlockSpec((1, D, BN), tile),
            pl.BlockSpec((1, D, BN), tile),
        ],
        out_specs=pl.BlockSpec((T, BN), lambda i: (0, i)),
        out_shape=sds((T, FF), BF),
        compiler_params=params(),
        cost_estimate=cost(2, 50e6),
        name="forward",
    )(a, w_gate, w_up)


def down_kernel(act_ref, w_ref, h_ref, out_ref, a_ref):
    h = h_ref[...] + mm(act_ref[...], w_ref[0], 1, 0).astype(BF)
    out_ref[...] = h
    a_ref[...] = normed(h)


def down(act, w_down, h, number, rows=256):
    return pl.pallas_call(
        down_kernel,
        grid=(T // rows,),
        in_specs=[
            pl.BlockSpec((rows, FF), lambda i: (i, 0)),
            pl.BlockSpec((1, FF, D), lambda i: (number, 0, 0)),
            pl.BlockSpec((rows, D), lambda i: (i, 0)),
        ],
        out_specs=[pl.BlockSpec((rows, D), lambda i: (i, 0))] * 2,
        out_shape=[sds((T, D), BF)] * 2,
        compiler_params=params(),
        cost_estimate=cost(1, 45e6),
        name="down",
    )(act, w_down, h)


def backward_kernel(rows, a_ref, dy_ref, g_ref, u_ref, d_ref, act_ref, dgate_ref, dup_ref):
    for r in range(0, T, rows):
        at = slice(r, r + rows)
        a = a_ref[at, :]
        gate = mm(a, g_ref[0], 1, 0)
        up = mm(a, u_ref[0], 1, 0)
        dact = mm(dy_ref[at, :], d_ref[0], 1, 1).astype(BF).astype(F32)
        sig = jax.nn.sigmoid(gate)
        silu = gate * sig
        act_ref[at, :] = (silu * up).astype(BF)
        dup_ref[at, :] = (dact * silu).astype(BF)
        dgate_ref[at, :] = (dact * up * (sig + silu * (1.0 - sig))).astype(BF)


def backward(a, dy, w_gate, w_up, w_down, number, wide=256):
    tile = lambda i: (number, 0, i)
    whole = pl.BlockSpec((T, D), lambda i: (0, 0))
    out = pl.BlockSpec((T, wide), lambda i: (0, i))
    return pl.pallas_call(
        functools.partial(backward_kernel, 512),
        grid=(FF // wide,),
        in_specs=[
            whole,
            whole,
            pl.BlockSpec((1, D, wide), tile),
            pl.BlockSpec((1, D, wide), tile),
            pl.BlockSpec((1, wide, D), lambda i: (number, i, 0)),
        ],
        out_specs=[out] * 3,
        out_shape=[sds((T, FF), BF)] * 3,
        compiler_params=params(),
        cost_estimate=cost(3, 110e6),
        name="backward",
    )(a, dy, w_gate, w_up, w_down)


def into_kernel(dg_ref, du_ref, g_ref, u_ref, h_ref, dy_ref, out_ref):
    da = mm(dg_ref[...], g_ref[0], 1, 1).astype(BF) + mm(du_ref[...], u_ref[0], 1, 1).astype(BF)
    da, h = da.astype(F32), h_ref[...].astype(F32)
    scale = lax.rsqrt(jnp.mean(h * h, -1, keepdims=True) + 1e-6)
    dh = scale * da - h * (scale * scale * scale) * jnp.mean(da * h, -1, keepdims=True)
    out_ref[...] = dy_ref[...] + dh.astype(BF)


def into(dgate, dup, w_gate, w_up, h, dy, number, rows=256):
    row = pl.BlockSpec((rows, D), lambda i: (i, 0))
    wide = pl.BlockSpec((rows, FF), lambda i: (i, 0))
    w = pl.BlockSpec((1, D, FF), lambda i: (number, 0, 0), pipeline_mode=pl.Buffered(1))
    return pl.pallas_call(
        into_kernel,
        grid=(T // rows,),
        in_specs=[wide, wide, w, w, row, row],
        out_specs=row,
        out_shape=sds((T, D), BF),
        compiler_params=params(),
        cost_estimate=cost(2, 80e6),
        name="into",
    )(dgate, dup, w_gate, w_up, h, dy)


ORDERS = ((4, 2, 1), (2, 1, 4), (1, 4, 2))


def place(j, order):
    first, second, third = order
    bit = lambda b: (j // b) % 2
    return bit(first), 2 * bit(second) + bit(third)


def wide_kernel(where_ref, a_ref, rhs_ref, own_ref, other_ref, flat, lhs):
    @pl.when(pl.program_id(0) == 0)
    def _():
        flat[...] = a_ref[...].T
        core = where_ref[8]
        for q in range(8):
            for side in range(2):
                block = 2 * where_ref[q] + (core if side == 0 else 1 - core)
                lhs[pl.ds(384 * side + 48 * q, 48), :] = flat[pl.ds(pl.multiple_of(block * 48, 16), 48), :]

    whole = mm(lhs[...], rhs_ref[...], 1, 0).astype(BF)
    own_ref[...] = whole[:384].reshape(8, 48, BN)
    other_ref[...] = whole[384:].reshape(8, 48, BN)


def wide_gradient(where, a, rhs):
    part = pl.BlockSpec((8, 48, BN), lambda i, w: (0, 0, i))
    return pl.pallas_call(
        wide_kernel,
        grid_spec=pltpu.PrefetchScalarGridSpec(
            num_scalar_prefetch=1,
            grid=(FF // BN,),
            in_specs=[pl.BlockSpec((T, D), lambda i, w: (0, 0)), pl.BlockSpec((T, BN), lambda i, w: (0, i))],
            out_specs=[part, part],
            scratch_shapes=[pltpu.VMEM((D, T), BF), pltpu.VMEM((D, T), BF)],
        ),
        out_shape=[sds((8, 48, FF), BF)] * 2,
        compiler_params=params(),
        cost_estimate=cost(1, 40e6),
        name="wide",
    )(where, a, rhs)


def tall_kernel(where_ref, act_ref, dy_ref, own_ref, other_ref, whole):
    core = where_ref[8]
    whole[...] = mm(act_ref[...], dy_ref[...], 0, 0).reshape(2, 384, D)
    own_ref[0] = whole[core].astype(BF)
    other_ref[0] = whole[1 - core].astype(BF)


def tall_gradient(where, act, dy):
    part = pl.BlockSpec((1, 384, D), lambda q, w: (q, 0, 0))
    return pl.pallas_call(
        tall_kernel,
        grid_spec=pltpu.PrefetchScalarGridSpec(
            num_scalar_prefetch=1,
            grid=(8,),
            in_specs=[pl.BlockSpec((T, 768), lambda q, w: (0, w[q])), pl.BlockSpec((T, D), lambda q, w: (0, 0))],
            out_specs=[part, part],
            scratch_shapes=[pltpu.VMEM((2, 384, D), F32)],
        ),
        out_shape=[sds((8, 384, D), BF)] * 2,
        compiler_params=params(),
        cost_estimate=cost(1, 40e6),
        name="tall",
    )(where, act, dy)


def pair_kernel(own_ref, got_ref, *refs):
    whole = (own_ref[0].astype(F32) + got_ref[0].astype(F32)).astype(BF)
    rows, columns = whole.shape
    for s in range(rows // 48):
        refs[-1][0, :, s * columns : (s + 1) * columns] = whole[s * 48 : (s + 1) * 48]


def pair_sum(own, got, side, old=None):
    n, r, c = own.shape
    block = pl.BlockSpec((1, r, c), lambda i: (i, 0, 0))
    return pl.pallas_call(
        pair_kernel,
        grid=(n,),
        in_specs=[block, block] + [pl.BlockSpec(memory_space=pl.ANY)] * (old is not None),
        out_specs=pl.BlockSpec((1, 48, FF), lambda i: (i, 0, side)),
        out_shape=sds((n, 48, 3 * FF), BF),
        input_output_aliases={2: 0} if old is not None else {},
        compiler_params=params(),
        cost_estimate=pl.CostEstimate(flops=int(4e8), bytes_accessed=6 * n * r * c, transcendentals=0),
        name="pair_sum",
    )(own, got, *((old,) if old is not None else ()))


def split_kernel(own_ref, got_ref, *refs):
    keeps, sends = refs[:3], refs[3:]
    whole = own_ref[...].astype(F32) + got_ref[...].astype(F32)

    def put(third, piece):
        for j in range(8):
            leaves, at = place(j, ORDERS[third])
            if leaves:
                sends[third][at] = piece[j].astype(BF)
            else:
                keeps[third][at] = piece[j]

    if whole.shape[1] == 48:
        for third in range(3):
            pl.when(pl.program_id(0) // 4 == third)(functools.partial(put, third, whole))
    else:
        for third in range(3):
            put(third, whole[:, :, third * 256 : third * 256 + 256])


def pair_split(own, got):
    _, r, c = own.shape
    if r == 48:
        grid, part = (12,), pl.BlockSpec((8, 48, BN), lambda i: (0, 0, i))
        out = [pl.BlockSpec((4, 48, BN), lambda i, k=k: (0, 0, jnp.clip(i - 4 * k, 0, 3))) for k in range(3)]
    else:
        grid, part = (8,), pl.BlockSpec((8, 48, c), lambda i: (0, i, 0))
        out = [pl.BlockSpec((4, 48, c // 3), lambda i: (0, i, 0))] * 3
        grid, part = (4,), pl.BlockSpec((8, 96, c), lambda i: (0, i, 0))
        out = [pl.BlockSpec((4, 96, c // 3), lambda i: (0, i, 0))] * 3
    return pl.pallas_call(
        split_kernel,
        grid=grid,
        in_specs=[part, part],
        out_specs=out * 2,
        out_shape=[sds((4, r, c // 3), F32)] * 3 + [sds((4, r, c // 3), BF)] * 3,
        compiler_params=params(),
        cost_estimate=pl.CostEstimate(flops=int(4e8), bytes_accessed=7 * 8 * r * c, transcendentals=0),
        name="pair_split",
    )(own, got)


def sum_kernel(n, *refs):
    keeps, gots, outs = refs[:3], refs[3:6], refs[6:]
    half = n // 2
    for k in range(3):
        if n == 1:
            c = keeps[k].shape[-1]
            outs[0][:, k * c : (k + 1) * c] = (keeps[k][0] + gots[k][0].astype(F32)).astype(BF)
        else:
            outs[k][...] = keeps[k][:half] + gots[k][:half].astype(F32)
            outs[3 + k][...] = (keeps[k][half:] + gots[k][half:].astype(F32)).astype(BF)


def add_step(keeps, gots):
    n, r, c = keeps[0].shape
    half = n // 2
    if n == 1:
        steps, rows = 1, r
        shapes = sds((r, 3 * c), BF)
        out_specs = pl.BlockSpec((r, 3 * c), lambda i: (0, 0))
    else:
        steps = 3
        rows = r // steps
        shapes = [sds((half, r, c), F32)] * 3 + [sds((half, r, c), BF)] * 3
        out_specs = [pl.BlockSpec((half, rows, c), lambda i: (0, i, 0))] * 6
    block = pl.BlockSpec((n, rows, c), lambda i: (0, i, 0))
    return pl.pallas_call(
        functools.partial(sum_kernel, n),
        grid=(steps,),
        in_specs=[block] * 6,
        out_specs=out_specs,
        out_shape=shapes,
        compiler_params=params(),
        cost_estimate=pl.CostEstimate(flops=int(4e7 * n), bytes_accessed=n * r * c * 30, transcendentals=0),
        name="add_step",
    )(*keeps, *gots)


def adamw_kernel(folded, w_ref, m_ref, v_ref, g_ref, *refs):
    nw, nm, nv = refs[-3:]

    def put(at, g):
        g = g.astype(F32)
        w = w_ref[0, at].astype(F32)
        m = 0.9 * m_ref[0, at] + 0.1 * g
        v = 0.95 * v_ref[0, at] + 0.05 * g * g
        step = m * lax.rsqrt(v + 1e-8) + 0.1 * w
        nw[0, at] = (w - 0.02 * step).astype(BF)
        nm[0, at] = m
        nv[0, at] = v

    if folded:
        for b in range(g_ref.shape[0] // 48):
            for s in range(8):
                put(pl.ds(b * 384 + s * 48, 48), g_ref[b * 48 : b * 48 + 48, s * D : s * D + D])
    else:
        put(slice(None), g_ref[...])


def adamw(w, m, v, g, number, old=None, side=0):
    _, r, c = w.shape
    folded = c != FF and g.shape[1] == 3 * FF
    steps = 8 if folded else 6
    block = pl.BlockSpec((1, r // steps, c), lambda i: (number, i, 0))
    g_block = (D // steps, FF) if folded else (r // steps, c)
    extra = tuple(old) if old is not None else ()
    return pl.pallas_call(
        functools.partial(adamw_kernel, folded),
        grid=(steps,),
        in_specs=[block] * 3 + [pl.BlockSpec(g_block, lambda i: (i, side))] + [pl.BlockSpec(memory_space=pl.ANY)] * len(extra),
        out_specs=[block] * 3,
        out_shape=[sds(w.shape, BF), sds(w.shape, F32), sds(w.shape, F32)],
        input_output_aliases={4 + i: i for i in range(len(extra))},
        compiler_params=params(),
        cost_estimate=pl.CostEstimate(flops=int(19e9), bytes_accessed=22 * r * c, transcendentals=r * c),
        name="adamw",
    )(w, m, v, g, *extra)


CHIPS, ALL = ("x", "y", "z"), ("x", "y", "z", "core")
NAME = {4: "x", 2: "y", 1: "z"}


def swap(x, axis):
    return lax.ppermute(x, axis, [(0, 1), (1, 0)])


def swap_step(sends, step):
    return [swap(s, NAME[order[step]]) for s, order in zip(sends, ORDERS)]


def gather(g):
    return lax.all_gather(g, ALL, axis=0, tiled=True)


def scatter(g):
    return lax.psum_scatter(g, CHIPS, scatter_dimension=0, tiled=True)[0]


def tie(x, after):
    return lax.optimization_barrier((x, after))[0]


class Line:
    def __init__(self):
        self.last = None

    def __call__(self, f, first, *rest, **kw):
        if self.last is not None:
            if isinstance(first, (list, tuple)):
                first = [tie(first[0], self.last), *first[1:]]
            else:
                first = tie(first, self.last)
        out = f(first, *rest, **kw)
        self.last = out[0] if isinstance(out, (list, tuple)) else out
        return out


def solution(mesh):
    split = jax.sharding.Mesh(mesh.devices.reshape(1, 2, 2, 2, 2), ("rep", *ALL))

    def step(x, dy, w_gate, w_up, w_down, m_gate, m_up, m_down, v_gate, v_up, v_down):
        x, dy = x[0], dy[0]
        chip = 4 * lax.axis_index("x") + 2 * lax.axis_index("y") + lax.axis_index("z")
        core = lax.axis_index("core")
        count = jnp.arange(8, dtype=jnp.int32)
        plain = jnp.concatenate([count, core[None].astype(jnp.int32)])
        nearest = jnp.concatenate([count ^ chip, core[None].astype(jnp.int32)])
        run = Line()
        wide = lambda rhs, a, where: wide_gradient(where, a, rhs)
        tall = lambda act, dy, where: tall_gradient(where, act, dy)

        a0 = normed(x)
        act0 = run(forward, a0, w_gate, w_up, 0)
        h1, a1 = run(down, act0, w_down, x, 0)
        act1, dgate1, dup1 = run(backward, a1, dy, w_gate, w_up, w_down, 1)

        d1, d1_other = run(tall, act1, dy, plain)
        d1_got = swap(d1_other, "core")
        g1, g1_other = run(wide, dgate1, a1, plain)
        g1_got = swap(g1_other, "core")
        u1, u1_other = run(wide, dup1, a1, plain)
        u1_got = swap(u1_other, "core")
        first = run(pair_sum, d1, d1_got, 2)
        first = run(pair_sum, g1, g1_got, 0, first)
        first = scatter(run(pair_sum, u1, u1_got, 1, first))
        by_h = run(into, dgate1, dup1, w_gate, w_up, h1, dy, 1)
        act0, dgate0, dup0 = run(backward, a0, by_h, w_gate, w_up, w_down, 0)
        first = gather(tie(first, act0))

        d0, d0_other = run(tall, act0, by_h, nearest)
        d0_got = swap(d0_other, "core")
        g0, g0_other = run(wide, dgate0, a0, nearest)
        g0_got = swap(g0_other, "core")
        d0 = run(pair_split, d0, d0_got)
        d0_in = swap_step(d0[3:], 0)
        u0, u0_other = run(wide, dup0, a0, nearest)
        u0_got = swap(u0_other, "core")
        g0 = run(pair_split, g0, g0_got)
        g0_in = swap_step(g0[3:], 0)
        u0 = run(pair_split, u0, u0_got)
        u0_in = swap_step(u0[3:], 0)
        d0 = run(add_step, d0[:3], d0_in)
        d0_in = swap_step(d0[3:], 1)
        new_d = run(adamw, w_down, m_down, v_down, first, 1, None, 2)
        d0 = run(add_step, d0[:3], d0_in)
        d0_in = swap_step(d0[3:], 2)
        g0 = run(add_step, g0[:3], g0_in)
        g0_in = swap_step(g0[3:], 1)
        u0 = run(add_step, u0[:3], u0_in)
        u0_in = swap_step(u0[3:], 1)
        d0 = gather(run(add_step, d0[:3], d0_in))
        new_g = run(adamw, w_gate, m_gate, v_gate, first, 1)
        g0 = run(add_step, g0[:3], g0_in)
        g0_in = swap_step(g0[3:], 2)
        u0 = run(add_step, u0[:3], u0_in)
        u0_in = swap_step(u0[3:], 2)
        g0 = gather(run(add_step, g0[:3], g0_in))
        new_u = run(adamw, w_up, m_up, v_up, first, 1, None, 1)
        u0 = gather(run(add_step, u0[:3], u0_in))
        new_d = run(adamw, w_down, m_down, v_down, d0, 0, new_d)
        new_g = run(adamw, w_gate, m_gate, v_gate, g0, 0, new_g)
        new_u = run(adamw, w_up, m_up, v_up, u0, 0, new_u)
        return tuple(one[which] for which in range(3) for one in (new_g, new_u, new_d))

    return jax.shard_map(
        step,
        mesh=split,
        in_specs=(P(("rep", *ALL), None, None),) * 2 + (P(None, None, None),) * 9,
        out_specs=(P("rep", None, None),) * 9,
        check_vma=False,
    )
```

time: 1260 us -> 827 us (0.66)
  Pallas kernels: 0 us -> 720 us
  matrix products: 521 us -> 0 us
  waiting for transfers between devices: 503 us -> 34 us
  other arithmetic: 206 us -> 7.37 us
  starting transfers between devices: 0.04 us -> 33.5 us
    pallas_call x0 -> x32, Pallas kernels: none -> 720 us  [the longest x6 202 us: adamw(): pl.pallas_call(functools.partial(adamw_kernel, folded), grid=(steps,), in...]
    dot_general x15 -> x0, matrix products: 521 us -> none  [the longest x5 194 us: layer(): gate = jnp.dot(a, w['w_gate'], preferred_element_type=jnp.float32)]
    psum x1 -> x0, waiting for transfers between devices: 503 us -> none  [step(): summed[number] = [lax.psum(by_w[name], 'dp') for name in NAMES]]
    convert_element_type x2 -> x1, other arithmetic: 200 us -> 4.13 us  [normed(): return (wide * scale).astype(BF)]
    ppermute x0 -> x33, waiting for transfers between devices: none -> 33.9 us  [swap(): return lax.ppermute(x, axis, [(0, 1), (1, 0)])]
    ppermute x0 -> x33, starting transfers between devices: none -> 33.3 us  [swap(): return lax.ppermute(x, axis, [(0, 1), (1, 0)])]
  transfers between devices with their start and end apart: 1 -> 38, of which waited for: 1 -> 6; matrix products, arithmetic and copies ran while one was open for 0% -> 0% of each run, Pallas kernels for 0% -> 62%
where the time goes in v1:
time: 827 us; the launch traced here: 816 us
  Pallas kernels  720 us (87%)
  waiting for transfers between devices  34 us (4%)
  starting transfers between devices  33.5 us (4%)
  between operations  14.6 us (2%)
    pallas_call x6, Pallas kernels, adamw(): pl.pallas_call(functools.partial(adamw_kernel, folded), grid=(steps,), in...  202 us
    pallas_call x2, Pallas kernels, backward(): pl.pallas_call(functools.partial(backward_kernel, 512), grid=(FF // wide,...  141 us
    pallas_call x4, Pallas kernels, wide_gradient(): pl.pallas_call(wide_kernel, grid_spec=pltpu.PrefetchScalarGridSpec(num_sc...  107 us
    pallas_call x2, Pallas kernels, tall_gradient(): pl.pallas_call(tall_kernel, grid_spec=pltpu.PrefetchScalarGridSpec(num_sc...  53.8 us
    pallas_call x1, Pallas kernels, into(): pl.pallas_call(into_kernel, grid=(T // rows,), in_specs=[wide, wide, w, w...  52.6 us
    pallas_call x1, Pallas kernels, forward(): pl.pallas_call(functools.partial(forward_kernel, 512), grid=(FF // BN,),...  45.2 us
    pallas_call x9, Pallas kernels, add_step(): pl.pallas_call(functools.partial(sum_kernel, n), grid=(steps,), in_specs=...  35.1 us
    ppermute x33, waiting for transfers between devices, swap(): return lax.ppermute(x, axis, [(0, 1), (1, 0)])  33.9 us
  transfers between devices with their start and end apart: 38, of which 6 were waited for; matrix products, arithmetic and copies ran while one was open for 0% of the time, Pallas kernels for 62%

profile of v1, /device:TPU:0, one launch (start us, length us, event | category | flops | bytes accessed | tf_op | source)
XLA Modules:
  0.0 815.8 jit_solution(3403433020876343773)
XLA Ops:
  9.8 4.1 fusion.1.a_ref
  13.9 45.2 %forward.1.act_ref = bf16[2048,6144]{1,0:T(8,128)(2,1)} custom-call(bf16[2048,768]{1,0:T(8,128)(2,1)} %fusion.1.a_ref, bf16[2,768,6144]{2,1,0:T(8,128)(2,1)} %w_ref.6, bf16[2,768,6144]{2,1,0:T(8,128)(2,1)} %w_ref.7), custom_call_target="tpu_custom_call" | custom-call | flops 38654705664 | bytes 50000000 | tf_op jit(solution)/shard_map/forward/pallas_call | solution.py:48
  59.2 28.3 %down.1 = (bf16[2048,768]{1,0:T(8,128)(2,1)}, bf16[2048,768]{1,0:T(8,128)(2,1)}) custom-call(bf16[2048,6144]{1,0:T(8,128)(2,1)} %forward.1.act_ref, bf16[2,6144,768]{2,1,0:T(8,128)(2,1)} %w_ref.5, bf16[2048,768]{1,0:T(8,128)(2,1)} %bitcast.6), custom_call_target="tpu_custom_call" | custom-call | flops 19327352832 | bytes 45000000 | tf_op jit(solution)/shard_map/down/pallas_call | solution.py:71
  87.5 70.5 %backward.2 = (bf16[2048,6144]{1,0:T(8,128)(2,1)}, bf16[2048,6144]{1,0:T(8,128)(2,1)}, bf16[2048,6144]{1,0:T(8,128)(2,1)}) custom-call(bf16[2048,768]{1,0:T(8,128)(2,1)} %get-tuple-element.133.a_ref, bf16[2048,768]{1,0:T(8,128)(2,1)} %bitcast.8, bf16[2,768,6144]{2,1,0:T(8,128)(2,1)} %w_ref.6, bf16[2,768,6144]{2,1,0:T(8,128)(2,1)} %w_ref.7, ...), custom_call_target="tpu_custom_call" | custom-call | flops 57982058496 | bytes 110000000 | tf_op jit(solution)/shard_map/backward/pallas_call | solution.py:105
  158.6 26.8 %tall.2 = (bf16[8,384,768]{2,1,0:T(8,128)(2,1)}, bf16[8,384,768]{2,1,0:T(8,128)(2,1)}) custom-call(s32[9]{0:T(128)} %get-tuple-element.254.where_ref, bf16[2048,6144]{1,0:T(8,128)(2,1)} %get-tuple-element.136.act_ref, bf16[2048,768]{1,0:T(8,128)(2,1)} %bitcast.9), custom_call_target="tpu_custom_call" | custom-call | flops 19327352832 | bytes 40000000 | tf_op jit(solution)/shard_map/tall/pallas_call | solution.py:198
  186.2 26.8 %wide.4 = (bf16[8,48,6144]{2,1,0:T(8,128)(2,1)}, bf16[8,48,6144]{2,1,0:T(8,128)(2,1)}) custom-call(s32[9]{0:T(128)} %get-tuple-element.254.where_ref, bf16[2048,768]{1,0:T(8,128)(2,1)} %get-tuple-element.133.a_ref, bf16[2048,6144]{1,0:T(8,128)(2,1)} %get-tuple-element.148.rhs_ref.dg_ref), custom_call_target="tpu_custom_call" | custom-call | flops 19327352832 | bytes 40000000 | tf_op jit(solution)/shard_map/wide/pallas_call | solution.py:173
  213.0 27.0 %wide.5 = (bf16[8,48,6144]{2,1,0:T(8,128)(2,1)}, bf16[8,48,6144]{2,1,0:T(8,128)(2,1)}) custom-call(s32[9]{0:T(128)} %get-tuple-element.254.where_ref, bf16[2048,768]{1,0:T(8,128)(2,1)} %get-tuple-element.133.a_ref, bf16[2048,6144]{1,0:T(8,128)(2,1)} %get-tuple-element.140.rhs_ref.du_ref), custom_call_target="tpu_custom_call" | custom-call | flops 19327352832 | bytes 40000000 | tf_op jit(solution)/shard_map/wide/pallas_call | solution.py:173
  240.5 8.2 %pair_sum.3.refs_0_ = bf16[8,48,18432]{2,1,0:T(8,128)(2,1)} custom-call(bf16[8,384,768]{2,1,0:T(8,128)(2,1)} %get-tuple-element.142.own_ref, bf16[8,384,768]{2,1,0:T(8,128)(2,1)} %collective-permute-done.got_ref), custom_call_target="tpu_custom_call" | custom-call | flops 400000000 | bytes 14155776 | tf_op jit(solution)/shard_map/pair_sum/pallas_call | solution.py:224
  248.7 8.2 %pair_sum.4.refs_0_ = bf16[8,48,18432]{2,1,0:T(8,128)(2,1)} custom-call(bf16[8,48,6144]{2,1,0:T(8,128)(2,1)} %get-tuple-element.144.own_ref, bf16[8,48,6144]{2,1,0:T(8,128)(2,1)} %collective-permute-done.1.got_ref, bf16[8,48,18432]{2,1,0:T(8,128)(2,1)} %pair_sum.3.refs_0_), custom_call_target="tpu_custom_call", output_to_operand_aliasing={{}: (2, {})} | custom-call | flops 400000000 | bytes 14155776 | tf_op jit(solution)/shard_map/pair_sum/pallas_call | solution.py:224
  256.9 8.2 %pair_sum.5 = bf16[8,48,18432]{2,1,0:T(8,128)(2,1)} custom-call(bf16[8,48,6144]{2,1,0:T(8,128)(2,1)} %get-tuple-element.146.own_ref, bf16[8,48,6144]{2,1,0:T(8,128)(2,1)} %collective-permute-done.2.got_ref, bf16[8,48,18432]{2,1,0:T(8,128)(2,1)} %pair_sum.4.refs_0_), custom_call_target="tpu_custom_call", output_to_operand_aliasing={{}: (2, {})} | custom-call | flops 400000000 | bytes 14155776 | tf_op jit(solution)/shard_map/pair_sum/pallas_call | solution.py:224
  265.2 52.6 %into.1.dy_ref = bf16[2048,768]{1,0:T(8,128)(2,1)} custom-call(bf16[2048,6144]{1,0:T(8,128)(2,1)} %get-tuple-element.148.rhs_ref.dg_ref, bf16[2048,6144]{1,0:T(8,128)(2,1)} %get-tuple-element.140.rhs_ref.du_ref, bf16[2,768,6144]{2,1,0:T(8,128)(2,1)} %w_ref.6, bf16[2,768,6144]{2,1,0:T(8,128)(2,1)} %w_ref.7, bf16[2048,768]{1,0:T(8,128)(2,1)} %get-tuple-element.132.h_ref, ...), custom_call_target="tpu_custom_call" | custom-call | flops 38654705664 | bytes 80000000 | tf_op jit(solution)/shard_map/into/pallas_call | solution.py:135
  317.7 70.4 %backward.3 = (bf16[2048,6144]{1,0:T(8,128)(2,1)}, bf16[2048,6144]{1,0:T(8,128)(2,1)}, bf16[2048,6144]{1,0:T(8,128)(2,1)}) custom-call(bf16[2048,768]{1,0:T(8,128)(2,1)} %fusion.1.a_ref, bf16[2048,768]{1,0:T(8,128)(2,1)} %into.1.dy_ref, bf16[2,768,6144]{2,1,0:T(8,128)(2,1)} %w_ref.6, bf16[2,768,6144]{2,1,0:T(8,128)(2,1)} %w_ref.7, bf16[2,6144,768]{2,1,0:T(8,128)(2,1)} %w_ref.5), custom_call_target="tpu_custom_call" | custom-call | flops 57982058496 | bytes 110000000 | tf_op jit(solution)/shard_map/backward/pallas_call | solution.py:105
  388.2 27.0 %tall.3 = (bf16[8,384,768]{2,1,0:T(8,128)(2,1)}, bf16[8,384,768]{2,1,0:T(8,128)(2,1)}) custom-call(s32[9]{0:T(128)} %get-tuple-element.253.where_ref, bf16[2048,6144]{1,0:T(8,128)(2,1)} %get-tuple-element.152.act_ref, bf16[2048,768]{1,0:T(8,128)(2,1)} %into.1.dy_ref), custom_call_target="tpu_custom_call" | custom-call | flops 19327352832 | bytes 40000000 | tf_op jit(solution)/shard_map/tall/pallas_call | solution.py:198
  415.2 26.8 %wide.6 = (bf16[8,48,6144]{2,1,0:T(8,128)(2,1)}, bf16[8,48,6144]{2,1,0:T(8,128)(2,1)}) custom-call(s32[9]{0:T(128)} %get-tuple-element.253.where_ref, bf16[2048,768]{1,0:T(8,128)(2,1)} %fusion.1.a_ref, bf16[2048,6144]{1,0:T(8,128)(2,1)} %get-tuple-element.155.rhs_ref), custom_call_target="tpu_custom_call" | custom-call | flops 19327352832 | bytes 40000000 | tf_op jit(solution)/shard_map/wide/pallas_call | solution.py:173
  442.5 7.0 pair_split.3
  449.5 26.8 %wide.7 = (bf16[8,48,6144]{2,1,0:T(8,128)(2,1)}, bf16[8,48,6144]{2,1,0:T(8,128)(2,1)}) custom-call(s32[9]{0:T(128)} %get-tuple-element.253.where_ref, bf16[2048,768]{1,0:T(8,128)(2,1)} %fusion.1.a_ref, bf16[2048,6144]{1,0:T(8,128)(2,1)} %get-tuple-element.160.rhs_ref), custom_call_target="tpu_custom_call" | custom-call | flops 19327352832 | bytes 40000000 | tf_op jit(solution)/shard_map/wide/pallas_call | solution.py:173
  482.4 11.4 %pair_split.4 = (f32[4,48,2048]{2,1,0:T(8,128)}, f32[4,48,2048]{2,1,0:T(8,128)}, f32[4,48,2048]{2,1,0:T(8,128)}, bf16[4,48,2048]{2,1,0:T(8,128)(2,1)}, bf16[4,48...) custom-call(bf16[8,48,6144]{2,1,0:T(8,128)(2,1)} %get-tuple-element.162.own_ref, ...), custom_call_target="tpu_custom_call" | custom-call | flops 400000000 | bytes 16515072 | tf_op jit(solution)/shard_map/pair_split/pallas_call | solution.py:267
  494.3 11.4 %pair_split.5 = (f32[4,48,2048]{2,1,0:T(8,128)}, f32[4,48,2048]{2,1,0:T(8,128)}, f32[4,48,2048]{2,1,0:T(8,128)}, bf16[4,48,2048]{2,1,0:T(8,128)(2,1)}, bf16[4,48...) custom-call(bf16[8,48,6144]{2,1,0:T(8,128)(2,1)} %get-tuple-element.165.own_ref, ...), custom_call_target="tpu_custom_call" | custom-call | flops 400000000 | bytes 16515072 | tf_op jit(solution)/shard_map/pair_split/pallas_call | solution.py:267
  505.7 8.9 %collective-permute-done.6.refs_3_ = bf16[4,384,256]{2,1,0:T(8,128)(2,1)S(1)} collective-permute-done((bf16[4,384,256]{2,1,0:T(8,128)(2,1)}, bf16[4,384,256]{2,1,0:T(8,128)(2,1)S(1)}, u32[]{:S(2)}, u32[]{:S(2)}) %collective-permute-start.6) | collective-permute-done | bytes 786464 | tf_op jit(solution)/shard_map/ppermute | solution.py:362
  518.4 5.5 add_step.9
  528.0 7.1 collective-permute-done.12.refs_3_
  537.2 6.3 collective-permute-done.11.refs_5_
  547.3 33.7 %adamw.6 = (bf16[2,6144,768]{2,1,0:T(8,128)(2,1)}, f32[2,6144,768]{2,1,0:T(8,128)}, f32[2,6144,768]{2,1,0:T(8,128)}) custom-call(bf16[2,6144,768]{2,1,0:T(8,128)(2,1)} %w_ref.5, f32[2,6144,768]{2,1,0:T(8,128)} %m_ref.9, f32[2,6144,768]{2,1,0:T(8,128)} %v_ref.9, bf16[768,18432]{1,0:T(8,128)(2,1)} %all-gather.5.cloned.1.call-done.g_ref), custom_call_target="tpu_custom_call" | custom-call | flops 19000000512 | bytes 103809024 | tf_op jit(solution)/shard_map/adamw/pallas_call | solution.py:344
  581.0 3.9 add_step.10
  586.5 5.5 add_step.11
  592.9 5.4 add_step.12
  607.2 8.6 %collective-permute-done.21.refs_3_ = bf16[2,48,2048]{2,1,0:T(8,128)(2,1)S(1)} collective-permute-done((bf16[2,48,2048]{2,1,0:T(8,128)(2,1)S(1)}, bf16[2,48,2048]{2,1,0:T(8,128)(2,1)S(1)}, u32[]{:S(2)}, u32[]{:S(2)}) %collective-permute-start.21) | collective-permute-done | bytes 393248 | tf_op jit(solution)/shard_map/ppermute | solution.py:362
  617.0 33.8 %adamw.7 = (bf16[2,768,6144]{2,1,0:T(8,128)(2,1)}, f32[2,768,6144]{2,1,0:T(8,128)}, f32[2,768,6144]{2,1,0:T(8,128)}) custom-call(bf16[2,768,6144]{2,1,0:T(8,128)(2,1)} %w_ref.6, f32[2,768,6144]{2,1,0:T(8,128)} %m_ref.10, f32[2,768,6144]{2,1,0:T(8,128)} %v_ref.10, bf16[768,18432]{1,0:T(8,128)(2,1)} %all-gather.5.cloned.1.call-done.g_ref), custom_call_target="tpu_custom_call" | custom-call | flops 19000000512 | bytes 103809024 | tf_op jit(solution)/shard_map/adamw/pallas_call | solution.py:344
  671.1 33.6 %adamw.8 = (bf16[2,768,6144]{2,1,0:T(8,128)(2,1)}, f32[2,768,6144]{2,1,0:T(8,128)}, f32[2,768,6144]{2,1,0:T(8,128)}) custom-call(bf16[2,768,6144]{2,1,0:T(8,128)(2,1)} %w_ref.7, f32[2,768,6144]{2,1,0:T(8,128)} %m_ref.11, f32[2,768,6144]{2,1,0:T(8,128)} %v_ref.11, bf16[768,18432]{1,0:T(8,128)(2,1)} %all-gather.5.cloned.1.call-done.g_ref), custom_call_target="tpu_custom_call" | custom-call | flops 19000000512 | bytes 103809024 | tf_op jit(solution)/shard_map/adamw/pallas_call | solution.py:344
  707.9 33.6 %adamw.9 = (bf16[2,6144,768]{2,1,0:T(8,128)(2,1)}, f32[2,6144,768]{2,1,0:T(8,128)}, f32[2,6144,768]{2,1,0:T(8,128)}) custom-call(bf16[2,6144,768]{2,1,0:T(8,128)(2,1)} %w_ref.5, f32[2,6144,768]{2,1,0:T(8,128)} %m_ref.9, f32[2,6144,768]{2,1,0:T(8,128)} %v_ref.9, ...), custom_call_target="tpu_custom_call", output_to_operand_aliasing={{0}: (4, {}), {1}: (5, {}), {2}: (6, {})} | custom-call | flops 19000000512 | bytes 103809024 | tf_op jit(solution)/shard_map/adamw/pallas_call | solution.py:344
  741.6 33.6 %adamw.10 = (bf16[2,768,6144]{2,1,0:T(8,128)(2,1)}, f32[2,768,6144]{2,1,0:T(8,128)}, f32[2,768,6144]{2,1,0:T(8,128)}) custom-call(bf16[2,768,6144]{2,1,0:T(8,128)(2,1)} %w_ref.6, f32[2,768,6144]{2,1,0:T(8,128)} %m_ref.10, f32[2,768,6144]{2,1,0:T(8,128)} %v_ref.10, ...), custom_call_target="tpu_custom_call", output_to_operand_aliasing={{0}: (4, {}), {1}: (5, {}), {2}: (6, {})} | custom-call | flops 19000000512 | bytes 103809024 | tf_op jit(solution)/shard_map/adamw/pallas_call | solution.py:344
  775.2 33.6 %adamw.11 = (bf16[2,768,6144]{2,1,0:T(8,128)(2,1)}, f32[2,768,6144]{2,1,0:T(8,128)}, f32[2,768,6144]{2,1,0:T(8,128)}) custom-call(bf16[2,768,6144]{2,1,0:T(8,128)(2,1)} %w_ref.7, f32[2,768,6144]{2,1,0:T(8,128)} %m_ref.11, f32[2,768,6144]{2,1,0:T(8,128)} %v_ref.11, ...), custom_call_target="tpu_custom_call", output_to_operand_aliasing={{0}: (4, {}), {1}: (5, {}), {2}: (6, {})} | custom-call | flops 19000000512 | bytes 103809024 | tf_op jit(solution)/shard_map/adamw/pallas_call | solution.py:344
  (139 shorter events, 61.5 us)
Async XLA Ops:
  7.2 380.9 %reduce-scatter.2.cloned.1.call-start = ((), (), s32[]{:S(2)}) async-start(), calls=%async_computation.1 | async-start | bytes 15925248 | tf_op jit(solution)/shard_map/reduce_scatter | solution.py:374
  185.4 55.0 %collective-permute-start = (bf16[8,384,768]{2,1,0:T(8,128)(2,1)}, bf16[8,384,768]{2,1,0:T(8,128)(2,1)}, u32[]{:S(2)}, u32[]{:S(2)}) collective-permute-start(bf16[8,384,768]{2,1,0:T(8,128)(2,1)} %get-tuple-element.143), channel_id=1, source_target_pairs={{0,1},{1,0},{2,3},{3,2},{4,5},{5,4},{6,7},{7,6},{8,9},{9,8},{10,11... | collective-permute-start | bytes 14155784 | tf_op jit(solution)/shard_map/ppermute | solution.py:362
  213.0 35.7 %collective-permute-start.1 = (bf16[8,48,6144]{2,1,0:T(8,128)(2,1)}, bf16[8,48,6144]{2,1,0:T(8,128)(2,1)}, u32[]{:S(2)}, u32[]{:S(2)}) collective-permute-start(bf16[8,48,6144]{2,1,0:T(8,128)(2,1)} %get-tuple-element.145), channel_id=1, source_target_pairs={{0,1},{1,0},{2,3},{3,2},{4,5},{5,4},{6,7},{7,6},{8,9},{9,8},{10,11... | collective-permute-start | bytes 14155784 | tf_op jit(solution)/shard_map/ppermute | solution.py:362
  240.0 16.9 %collective-permute-start.2 = (bf16[8,48,6144]{2,1,0:T(8,128)(2,1)}, bf16[8,48,6144]{2,1,0:T(8,128)(2,1)}, u32[]{:S(2)}, u32[]{:S(2)}) collective-permute-start(bf16[8,48,6144]{2,1,0:T(8,128)(2,1)} %get-tuple-element.147), channel_id=1, source_target_pairs={{0,1},{1,0},{2,3},{3,2},{4,5},{5,4},{6,7},{7,6},{8,9},{9,8},{10,11... | collective-permute-start | bytes 14155784 | tf_op jit(solution)/shard_map/ppermute | solution.py:362
  265.1 282.2 %all-gather.5.cloned.1.call-start = ((), (), s32[]{:S(2)}) async-start(), calls=%async_computation.2 | async-start | bytes 30081024 | tf_op jit(solution)/shard_map/all_gather | solution.py:370
  388.1 319.8 %all-gather.7.cloned.1.call-start = ((), (), s32[]{:S(2)}) async-start(), calls=%async_computation.3 | async-start | bytes 10027008 | tf_op jit(solution)/shard_map/all_gather | solution.py:370
  415.2 27.3 %collective-permute-start.3 = (bf16[8,384,768]{2,1,0:T(8,128)(2,1)}, bf16[8,384,768]{2,1,0:T(8,128)(2,1)}, u32[]{:S(2)}, u32[]{:S(2)}) collective-permute-start(bf16[8,384,768]{2,1,0:T(8,128)(2,1)} %get-tuple-element.158), channel_id=1, source_target_pairs={{0,1},{1,0},{2,3},{3,2},{4,5},{5,4},{6,7},{7,6},{8,9},{9,8},{10,11... | collective-permute-start | bytes 14155784 | tf_op jit(solution)/shard_map/ppermute | solution.py:362
  442.0 40.4 %collective-permute-start.4 = (bf16[8,48,6144]{2,1,0:T(8,128)(2,1)}, bf16[8,48,6144]{2,1,0:T(8,128)(2,1)}, u32[]{:S(2)}, u32[]{:S(2)}) collective-permute-start(bf16[8,48,6144]{2,1,0:T(8,128)(2,1)} %get-tuple-element.163), channel_id=1, source_target_pairs={{0,1},{1,0},{2,3},{3,2},{4,5},{5,4},{6,7},{7,6},{8,9},{9,8},{10,11... | collective-permute-start | bytes 14155784 | tf_op jit(solution)/shard_map/ppermute | solution.py:362
  476.3 18.0 %collective-permute-start.5 = (bf16[8,48,6144]{2,1,0:T(8,128)(2,1)}, bf16[8,48,6144]{2,1,0:T(8,128)(2,1)}, u32[]{:S(2)}, u32[]{:S(2)}) collective-permute-start(bf16[8,48,6144]{2,1,0:T(8,128)(2,1)} %get-tuple-element.166), channel_id=1, source_target_pairs={{0,1},{1,0},{2,3},{3,2},{4,5},{5,4},{6,7},{7,6},{8,9},{9,8},{10,11... | collective-permute-start | bytes 14155784 | tf_op jit(solution)/shard_map/ppermute | solution.py:362
  476.3 38.2 %collective-permute-start.6 = (bf16[4,384,256]{2,1,0:T(8,128)(2,1)}, bf16[4,384,256]{2,1,0:T(8,128)(2,1)S(1)}, u32[]{:S(2)}, u32[]{:S(2)}) collective-permute-start(bf16[4,384,256]{2,1,0:T(8,128)(2,1)} %get-tuple-element.171), channel_id=1, source_target_pairs={{0,8},{8,0},{1,9},{9,1},{2,10},{10,2},{3,11},{11,3},{4,12},{12,4},... | collective-permute-start | bytes 2359304 | tf_op jit(solution)/shard_map/ppermute | solution.py:362
  479.3 36.9 %collective-permute-start.7 = (bf16[4,384,256]{2,1,0:T(8,128)(2,1)}, bf16[4,384,256]{2,1,0:T(8,128)(2,1)S(1)}, u32[]{:S(2)}, u32[]{:S(2)}) collective-permute-start(bf16[4,384,256]{2,1,0:T(8,128)(2,1)} %get-tuple-element.172), channel_id=1, source_target_pairs={{0,4},{4,0},{1,5},{5,1},{2,6},{6,2},{3,7},{7,3},{8,12},{12,8},{9,1... | collective-permute-start | bytes 2359304 | tf_op jit(solution)/shard_map/ppermute | solution.py:362
  480.8 36.7 %collective-permute-start.8 = (bf16[4,384,256]{2,1,0:T(8,128)(2,1)}, bf16[4,384,256]{2,1,0:T(8,128)(2,1)S(1)}, u32[]{:S(2)}, u32[]{:S(2)}) collective-permute-start(bf16[4,384,256]{2,1,0:T(8,128)(2,1)} %get-tuple-element.173), channel_id=1, source_target_pairs={{0,2},{2,0},{1,3},{3,1},{4,6},{6,4},{5,7},{7,5},{8,10},{10,8},{9,1... | collective-permute-start | bytes 2359304 | tf_op jit(solution)/shard_map/ppermute | solution.py:362
  493.8 41.3 %collective-permute-start.12 = (bf16[4,48,2048]{2,1,0:T(8,128)(2,1)}, bf16[4,48,2048]{2,1,0:T(8,128)(2,1)S(1)}, u32[]{:S(2)}, u32[]{:S(2)}) collective-permute-start(bf16[4,48,2048]{2,1,0:T(8,128)(2,1)} %get-tuple-element.188), channel_id=1, source_target_pairs={{0,8},{8,0},{1,9},{9,1},{2,10},{10,2},{3,11},{11,3},{4,12},{12,4},... | collective-permute-start | bytes 2359304 | tf_op jit(solution)/shard_map/ppermute | solution.py:362
  524.8 18.8 %collective-permute-start.11 = (bf16[2,384,256]{2,1,0:T(8,128)(2,1)}, bf16[2,384,256]{2,1,0:T(8,128)(2,1)S(1)}, u32[]{:S(2)}, u32[]{:S(2)}) collective-permute-start(bf16[2,384,256]{2,1,0:T(8,128)(2,1)} %get-tuple-element.183), channel_id=1, source_target_pairs={{0,8},{8,0},{1,9},{9,1},{2,10},{10,2},{3,11},{11,3},{4,12},{12,4},... | collective-permute-start | bytes 1179656 | tf_op jit(solution)/shard_map/ppermute | solution.py:362
  526.0 19.9 %collective-permute-start.9 = (bf16[2,384,256]{2,1,0:T(8,128)(2,1)}, bf16[2,384,256]{2,1,0:T(8,128)(2,1)}, u32[]{:S(2)}, u32[]{:S(2)}) collective-permute-start(bf16[2,384,256]{2,1,0:T(8,128)(2,1)} %get-tuple-element.181), channel_id=1, source_target_pairs={{0,4},{4,0},{1,5},{5,1},{2,6},{6,2},{3,7},{7,3},{8,12},{12,8},{9,1... | collective-permute-start | bytes 1179656 | tf_op jit(solution)/shard_map/ppermute | solution.py:362
  526.6 58.4 %collective-permute-start.13 = (bf16[4,48,2048]{2,1,0:T(8,128)(2,1)}, bf16[4,48,2048]{2,1,0:T(8,128)(2,1)S(1)}, u32[]{:S(2)}, u32[]{:S(2)}) collective-permute-start(bf16[4,48,2048]{2,1,0:T(8,128)(2,1)} %get-tuple-element.189), channel_id=1, source_target_pairs={{0,4},{4,0},{1,5},{5,1},{2,6},{6,2},{3,7},{7,3},{8,12},{12,8},{9,1... | collective-permute-start | bytes 2359304 | tf_op jit(solution)/shard_map/ppermute | solution.py:362
  535.1 50.4 %collective-permute-start.14 = (bf16[4,48,2048]{2,1,0:T(8,128)(2,1)}, bf16[4,48,2048]{2,1,0:T(8,128)(2,1)}, u32[]{:S(2)}, u32[]{:S(2)}) collective-permute-start(bf16[4,48,2048]{2,1,0:T(8,128)(2,1)} %get-tuple-element.190), channel_id=1, source_target_pairs={{0,2},{2,0},{1,3},{3,1},{4,6},{6,4},{5,7},{7,5},{8,10},{10,8},{9,1... | collective-permute-start | bytes 2359304 | tf_op jit(solution)/shard_map/ppermute | solution.py:362
  536.7 49.4 %collective-permute-start.15 = (bf16[4,48,2048]{2,1,0:T(8,128)(2,1)}, bf16[4,48,2048]{2,1,0:T(8,128)(2,1)S(1)}, u32[]{:S(2)}, u32[]{:S(2)}) collective-permute-start(bf16[4,48,2048]{2,1,0:T(8,128)(2,1)} %get-tuple-element.195), channel_id=1, source_target_pairs={{0,8},{8,0},{1,9},{9,1},{2,10},{10,2},{3,11},{11,3},{4,12},{12,4},... | collective-permute-start | bytes 2359304 | tf_op jit(solution)/shard_map/ppermute | solution.py:362
  544.3 47.7 %collective-permute-start.16 = (bf16[4,48,2048]{2,1,0:T(8,128)(2,1)}, bf16[4,48,2048]{2,1,0:T(8,128)(2,1)S(1)}, u32[]{:S(2)}, u32[]{:S(2)}) collective-permute-start(bf16[4,48,2048]{2,1,0:T(8,128)(2,1)} %get-tuple-element.196), channel_id=1, source_target_pairs={{0,4},{4,0},{1,5},{5,1},{2,6},{6,2},{3,7},{7,3},{8,12},{12,8},{9,1... | collective-permute-start | bytes 2359304 | tf_op jit(solution)/shard_map/ppermute | solution.py:362
  545.9 46.1 %collective-permute-start.17 = (bf16[4,48,2048]{2,1,0:T(8,128)(2,1)}, bf16[4,48,2048]{2,1,0:T(8,128)(2,1)}, u32[]{:S(2)}, u32[]{:S(2)}) collective-permute-start(bf16[4,48,2048]{2,1,0:T(8,128)(2,1)} %get-tuple-element.197), channel_id=1, source_target_pairs={{0,2},{2,0},{1,3},{3,1},{4,6},{6,4},{5,7},{7,5},{8,10},{10,8},{9,1... | collective-permute-start | bytes 2359304 | tf_op jit(solution)/shard_map/ppermute | solution.py:362
  585.0 13.3 %collective-permute-start.18 = (bf16[1,384,256]{2,1,0:T(8,128)(2,1)}, bf16[1,384,256]{2,1,0:T(8,128)(2,1)S(1)}, u32[]{:S(2)}, u32[]{:S(2)}) collective-permute-start(bf16[1,384,256]{2,1,0:T(8,128)(2,1)} %get-tuple-element.202), channel_id=1, source_target_pairs={{0,2},{2,0},{1,3},{3,1},{4,6},{6,4},{5,7},{7,5},{8,10},{10,8},{9,1... | collective-permute-start | bytes 589832 | tf_op jit(solution)/shard_map/ppermute | solution.py:362
  601.5 140.1 %all-gather.9.cloned.1.call-start = ((), (), s32[]{:S(2)}) async-start(), calls=%async_computation.4 | async-start | bytes 10027008 | tf_op jit(solution)/shard_map/all_gather | solution.py:370
  601.5 14.3 %collective-permute-start.21 = (bf16[2,48,2048]{2,1,0:T(8,128)(2,1)S(1)}, bf16[2,48,2048]{2,1,0:T(8,128)(2,1)S(1)}, u32[]{:S(2)}, u32[]{:S(2)}) collective-permute-start(bf16[2,48,2048]{2,1,0:T(8,128)(2,1)S(1)} %copy-done.25), channel_id=1, source_target_pairs={{0,4},{4,0},{1,5},{5,1},{2,6},{6,2},{3,7},{7,3},{8,12},{12,8},{9,1... | collective-permute-start | bytes 1179656 | tf_op jit(solution)/shard_map/ppermute | solution.py:362
  603.2 47.6 %collective-permute-start.22 = (bf16[2,48,2048]{2,1,0:T(8,128)(2,1)}, bf16[2,48,2048]{2,1,0:T(8,128)(2,1)S(1)}, u32[]{:S(2)}, u32[]{:S(2)}) collective-permute-start(bf16[2,48,2048]{2,1,0:T(8,128)(2,1)} %get-tuple-element.211), channel_id=1, source_target_pairs={{0,2},{2,0},{1,3},{3,1},{4,6},{6,4},{5,7},{7,5},{8,10},{10,8},{9,1... | collective-permute-start | bytes 1179656 | tf_op jit(solution)/shard_map/ppermute | solution.py:362
  604.7 46.1 %collective-permute-start.23 = (bf16[2,48,2048]{2,1,0:T(8,128)(2,1)S(1)}, bf16[2,48,2048]{2,1,0:T(8,128)(2,1)S(1)}, u32[]{:S(2)}, u32[]{:S(2)}) collective-permute-start(bf16[2,48,2048]{2,1,0:T(8,128)(2,1)S(1)} %copy-done.24), channel_id=1, source_target_pairs={{0,8},{8,0},{1,9},{9,1},{2,10},{10,2},{3,11},{11,3},{4,12},{12,4},... | collective-permute-start | bytes 1179656 | tf_op jit(solution)/shard_map/ppermute | solution.py:362
  606.2 51.7 %collective-permute-start.24 = (bf16[2,48,2048]{2,1,0:T(8,128)(2,1)}, bf16[2,48,2048]{2,1,0:T(8,128)(2,1)S(1)}, u32[]{:S(2)}, u32[]{:S(2)}) collective-permute-start(bf16[2,48,2048]{2,1,0:T(8,128)(2,1)} %get-tuple-element.217), channel_id=1, source_target_pairs={{0,4},{4,0},{1,5},{5,1},{2,6},{6,2},{3,7},{7,3},{8,12},{12,8},{9,1... | collective-permute-start | bytes 1179656 | tf_op jit(solution)/shard_map/ppermute | solution.py:362
  606.7 53.5 %collective-permute-start.25 = (bf16[2,48,2048]{2,1,0:T(8,128)(2,1)}, bf16[2,48,2048]{2,1,0:T(8,128)(2,1)S(1)}, u32[]{:S(2)}, u32[]{:S(2)}) collective-permute-start(bf16[2,48,2048]{2,1,0:T(8,128)(2,1)} %get-tuple-element.218), channel_id=1, source_target_pairs={{0,2},{2,0},{1,3},{3,1},{4,6},{6,4},{5,7},{7,5},{8,10},{10,8},{9,1... | collective-permute-start | bytes 1179656 | tf_op jit(solution)/shard_map/ppermute | solution.py:362
  615.8 44.4 %collective-permute-start.26 = (bf16[2,48,2048]{2,1,0:T(8,128)(2,1)}, bf16[2,48,2048]{2,1,0:T(8,128)(2,1)S(1)}, u32[]{:S(2)}, u32[]{:S(2)}) collective-permute-start(bf16[2,48,2048]{2,1,0:T(8,128)(2,1)} %get-tuple-element.219), channel_id=1, source_target_pairs={{0,8},{8,0},{1,9},{9,1},{2,10},{10,2},{3,11},{11,3},{4,12},{12,4},... | collective-permute-start | bytes 1179656 | tf_op jit(solution)/shard_map/ppermute | solution.py:362
  668.3 107.0 %all-gather.11.cloned.1.call-start = ((), (), s32[]{:S(2)}) async-start(), calls=%async_computation.5 | async-start | bytes 10027008 | tf_op jit(solution)/shard_map/all_gather | solution.py:370
  668.3 36.4 %collective-permute-start.30 = (bf16[1,48,2048]{2,1,0:T(8,128)(2,1)}, bf16[1,48,2048]{2,1,0:T(8,128)(2,1)S(1)}, u32[]{:S(2)}, u32[]{:S(2)}) collective-permute-start(bf16[1,48,2048]{2,1,0:T(8,128)(2,1)} %get-tuple-element.232), channel_id=1, source_target_pairs={{0,2},{2,0},{1,3},{3,1},{4,6},{6,4},{5,7},{7,5},{8,10},{10,8},{9,1... | collective-permute-start | bytes 589832 | tf_op jit(solution)/shard_map/ppermute | solution.py:362
  669.2 35.5 %collective-permute-start.31 = (bf16[1,48,2048]{2,1,0:T(8,128)(2,1)}, bf16[1,48,2048]{2,1,0:T(8,128)(2,1)S(1)}, u32[]{:S(2)}, u32[]{:S(2)}) collective-permute-start(bf16[1,48,2048]{2,1,0:T(8,128)(2,1)} %get-tuple-element.233), channel_id=1, source_target_pairs={{0,8},{8,0},{1,9},{9,1},{2,10},{10,2},{3,11},{11,3},{4,12},{12,4},... | collective-permute-start | bytes 589832 | tf_op jit(solution)/shard_map/ppermute | solution.py:362
  670.4 34.4 %collective-permute-start.32 = (bf16[1,48,2048]{2,1,0:T(8,128)(2,1)}, bf16[1,48,2048]{2,1,0:T(8,128)(2,1)S(1)}, u32[]{:S(2)}, u32[]{:S(2)}) collective-permute-start(bf16[1,48,2048]{2,1,0:T(8,128)(2,1)} %get-tuple-element.234), channel_id=1, source_target_pairs={{0,4},{4,0},{1,5},{5,1},{2,6},{6,2},{3,7},{7,3},{8,12},{12,8},{9,1... | collective-permute-start | bytes 589832 | tf_op jit(solution)/shard_map/ppermute | solution.py:362
  (32 other events, 236.3 us)
Sparse Core Ops, SparseCore 0:
  265.2 114.3 reduce-scatter.1
  388.2 136.8 all-gather.4
  601.6 59.9 all-gather.6
  668.4 51.2 all-gather.8
  721.8 52.0 all-gather.10

commit v2 on v1

--- a/solution.py
+++ b/solution.py
@@ -35,12 +35,13 @@
     return lax.dot_general(a, b, (((ca,), (cb,)), ((), ())), preferred_element_type=F32)
 
 
-def forward_kernel(rows, a_ref, g_ref, u_ref, act_ref):
+def forward_kernel(rows, a_ref, g_ref, u_ref, act_ref, gate_ref):
     for r in range(0, T, rows):
         a = a_ref[r : r + rows, :]
         gate = mm(a, g_ref[0], 1, 0)
         up = mm(a, u_ref[0], 1, 0)
         act_ref[r : r + rows, :] = (gate * jax.nn.sigmoid(gate) * up).astype(BF)
+        gate_ref[r : r + rows, :] = gate
 
 
 def forward(a, w_gate, w_up, number):
@@ -53,10 +54,10 @@
             pl.BlockSpec((1, D, BN), tile),
             pl.BlockSpec((1, D, BN), tile),
         ],
-        out_specs=pl.BlockSpec((T, BN), lambda i: (0, i)),
-        out_shape=sds((T, FF), BF),
-        compiler_params=params(),
-        cost_estimate=cost(2, 50e6),
+        out_specs=[pl.BlockSpec((T, BN), lambda i: (0, i))] * 2,
+        out_shape=[sds((T, FF), BF), sds((T, FF), F32)],
+        compiler_params=params(),
+        cost_estimate=cost(2, 100e6),
         name="forward",
     )(a, w_gate, w_up)
 
@@ -120,6 +121,39 @@
     )(a, dy, w_gate, w_up, w_down)
 
 
+def kept_kernel(rows, a_ref, dy_ref, gate_ref, u_ref, d_ref, dgate_ref, dup_ref):
+    for r in range(0, T, rows):
+        at = slice(r, r + rows)
+        gate = gate_ref[at, :]
+        up = mm(a_ref[at, :], u_ref[0], 1, 0)
+        dact = mm(dy_ref[at, :], d_ref[0], 1, 1).astype(BF).astype(F32)
+        sig = jax.nn.sigmoid(gate)
+        silu = gate * sig
+        dup_ref[at, :] = (dact * silu).astype(BF)
+        dgate_ref[at, :] = (dact * up * (sig + silu * (1.0 - sig))).astype(BF)
+
+
+def backward_kept(a, dy, gate, w_up, w_down, number, wide=256):
+    whole = pl.BlockSpec((T, D), lambda i: (0, 0))
+    out = pl.BlockSpec((T, wide), lambda i: (0, i))
+    return pl.pallas_call(
+        functools.partial(kept_kernel, 512),
+        grid=(FF // wide,),
+        in_specs=[
+            whole,
+            whole,
+            out,
+            pl.BlockSpec((1, D, wide), lambda i: (number, 0, i)),
+            pl.BlockSpec((1, wide, D), lambda i: (number, i, 0)),
+        ],
+        out_specs=[out] * 2,
+        out_shape=[sds((T, FF), BF)] * 2,
+        compiler_params=params(),
+        cost_estimate=cost(2, 130e6),
+        name="backward_kept",
+    )(a, dy, gate, w_up, w_down)
+
+
 def into_kernel(dg_ref, du_ref, g_ref, u_ref, h_ref, dy_ref, out_ref):
     da = mm(dg_ref[...], g_ref[0], 1, 1).astype(BF) + mm(du_ref[...], u_ref[0], 1, 1).astype(BF)
     da, h = da.astype(F32), h_ref[...].astype(F32)
@@ -234,6 +268,25 @@
     )(own, got, *((old,) if old is not None else ()))
 
 
+def one_kernel(own_ref, got_ref, out_ref):
+    out_ref[...] = (own_ref[...].astype(F32) + got_ref[...].astype(F32)).astype(BF)
+
+
+def pair_one(own, got):
+    n, r, c = own.shape
+    block = pl.BlockSpec((2, r, c), lambda i: (i, 0, 0))
+    return pl.pallas_call(
+        one_kernel,
+        grid=(n // 2,),
+        in_specs=[block, block],
+        out_specs=block,
+        out_shape=sds((n, r, c), BF),
+        compiler_params=params(),
+        cost_estimate=pl.CostEstimate(flops=int(4e8), bytes_accessed=6 * n * r * c, transcendentals=0),
+        name="pair_one",
+    )(own, got)
+
+
 def split_kernel(own_ref, got_ref, *refs):
     keeps, sends = refs[:3], refs[3:]
     whole = own_ref[...].astype(F32) + got_ref[...].astype(F32)
@@ -246,24 +299,14 @@
             else:
                 keeps[third][at] = piece[j]
 
-    if whole.shape[1] == 48:
-        for third in range(3):
-            pl.when(pl.program_id(0) // 4 == third)(functools.partial(put, third, whole))
-    else:
-        for third in range(3):
-            put(third, whole[:, :, third * 256 : third * 256 + 256])
+    for third in range(3):
+        pl.when(pl.program_id(0) // 2 == third)(functools.partial(put, third, whole))
 
 
 def pair_split(own, got):
     _, r, c = own.shape
-    if r == 48:
-        grid, part = (12,), pl.BlockSpec((8, 48, BN), lambda i: (0, 0, i))
-        out = [pl.BlockSpec((4, 48, BN), lambda i, k=k: (0, 0, jnp.clip(i - 4 * k, 0, 3))) for k in range(3)]
-    else:
-        grid, part = (8,), pl.BlockSpec((8, 48, c), lambda i: (0, i, 0))
-        out = [pl.BlockSpec((4, 48, c // 3), lambda i: (0, i, 0))] * 3
-        grid, part = (4,), pl.BlockSpec((8, 96, c), lambda i: (0, i, 0))
-        out = [pl.BlockSpec((4, 96, c // 3), lambda i: (0, i, 0))] * 3
+    grid, part = (6,), pl.BlockSpec((8, 48, 1024), lambda i: (0, 0, i))
+    out = [pl.BlockSpec((4, 48, 1024), lambda i, k=k: (0, 0, jnp.clip(i - 2 * k, 0, 1))) for k in range(3)]
     return pl.pallas_call(
         split_kernel,
         grid=grid,
@@ -408,7 +451,7 @@
         tall = lambda act, dy, where: tall_gradient(where, act, dy)
 
         a0 = normed(x)
-        act0 = run(forward, a0, w_gate, w_up, 0)
+        act0, gate0 = run(forward, a0, w_gate, w_up, 0)
         h1, a1 = run(down, act0, w_down, x, 0)
         act1, dgate1, dup1 = run(backward, a1, dy, w_gate, w_up, w_down, 1)
 
@@ -422,37 +465,34 @@
         first = run(pair_sum, g1, g1_got, 0, first)
         first = scatter(run(pair_sum, u1, u1_got, 1, first))
         by_h = run(into, dgate1, dup1, w_gate, w_up, h1, dy, 1)
-        act0, dgate0, dup0 = run(backward, a0, by_h, w_gate, w_up, w_down, 0)
-        first = gather(tie(first, act0))
-
-        d0, d0_other = run(tall, act0, by_h, nearest)
+        dgate0, dup0 = run(backward_kept, a0, by_h, gate0, w_up, w_down, 0)
+        first = gather(tie(first, dgate0))
+
+        d0, d0_other = run(tall, act0, by_h, plain)
         d0_got = swap(d0_other, "core")
         g0, g0_other = run(wide, dgate0, a0, nearest)
         g0_got = swap(g0_other, "core")
-        d0 = run(pair_split, d0, d0_got)
-        d0_in = swap_step(d0[3:], 0)
+        d0 = run(pair_one, d0, d0_got)
         u0, u0_other = run(wide, dup0, a0, nearest)
         u0_got = swap(u0_other, "core")
         g0 = run(pair_split, g0, g0_got)
         g0_in = swap_step(g0[3:], 0)
         u0 = run(pair_split, u0, u0_got)
         u0_in = swap_step(u0[3:], 0)
-        d0 = run(add_step, d0[:3], d0_in)
-        d0_in = swap_step(d0[3:], 1)
-        new_d = run(adamw, w_down, m_down, v_down, first, 1, None, 2)
-        d0 = run(add_step, d0[:3], d0_in)
-        d0_in = swap_step(d0[3:], 2)
         g0 = run(add_step, g0[:3], g0_in)
         g0_in = swap_step(g0[3:], 1)
+        d0 = scatter(tie(tie(d0, run.last), first))
+        new_d = run(adamw, w_down, m_down, v_down, first, 1, None, 2)
         u0 = run(add_step, u0[:3], u0_in)
         u0_in = swap_step(u0[3:], 1)
-        d0 = gather(run(add_step, d0[:3], d0_in))
-        new_g = run(adamw, w_gate, m_gate, v_gate, first, 1)
         g0 = run(add_step, g0[:3], g0_in)
         g0_in = swap_step(g0[3:], 2)
+        run.last = d0
+        d0 = gather(tie(d0, g0[0]))
+        new_g = run(adamw, w_gate, m_gate, v_gate, first, 1)
+        g0 = gather(run(add_step, g0[:3], g0_in))
         u0 = run(add_step, u0[:3], u0_in)
         u0_in = swap_step(u0[3:], 2)
-        g0 = gather(run(add_step, g0[:3], g0_in))
         new_u = run(adamw, w_up, m_up, v_up, first, 1, None, 1)
         u0 = gather(run(add_step, u0[:3], u0_in))
         new_d = run(adamw, w_down, m_down, v_down, d0, 0, new_d)

time: 827 us -> 822 us (level)
  waiting for transfers between devices: 34 us -> 68.3 us
  Pallas kernels: 720 us -> 693 us
  starting transfers between devices: 33.5 us -> 21.3 us
    pallas_call x2 -> x1, Pallas kernels: 141 us -> 70.5 us  [backward(): pl.pallas_call(functools.partial(backward_kernel, 512), grid=(FF // wide,...]
    pallas_call x0 -> x2, Pallas kernels: none -> 65.8 us  [the longest x1 59.4 us: backward_kept(): pl.pallas_call(functools.partial(kept_kernel, 512), grid=(FF // wide,), i...]
    ppermute x33 -> x24, waiting for transfers between devices: 33.9 us -> 65.7 us  [swap(): return lax.ppermute(x, axis, [(0, 1), (1, 0)])]
    ppermute x33 -> x24, starting transfers between devices: 33.3 us -> 21 us  [swap(): return lax.ppermute(x, axis, [(0, 1), (1, 0)])]
    pallas_call x3 -> x2, Pallas kernels: 29.8 us -> 17.7 us  [pair_split(): pl.pallas_call(split_kernel, grid=grid, in_specs=[part, part], out_specs=...]
    pallas_call x9 -> x6, Pallas kernels: 35.1 us -> 23.5 us  [add_step(): pl.pallas_call(functools.partial(sum_kernel, n), grid=(steps,), in_specs=...]
  transfers between devices with their start and end apart: 38 -> 30, of which waited for: 6 -> 4; matrix products, arithmetic and copies ran while one was open for 0% -> 0% of each run, Pallas kernels for 62% -> 59%
where the time goes in v2:
time: 822 us; the launch traced here: 810 us
  Pallas kernels  693 us (84%)
  waiting for transfers between devices  68.3 us (8%)
  starting transfers between devices  21.3 us (3%)
  between operations  14.8 us (2%)
    pallas_call x6, Pallas kernels, adamw(): pl.pallas_call(functools.partial(adamw_kernel, folded), grid=(steps,), in...  202 us
    pallas_call x4, Pallas kernels, wide_gradient(): pl.pallas_call(wide_kernel, grid_spec=pltpu.PrefetchScalarGridSpec(num_sc...  107 us
    pallas_call x1, Pallas kernels, backward(): pl.pallas_call(functools.partial(backward_kernel, 512), grid=(FF // wide,...  70.5 us
    ppermute x24, waiting for transfers between devices, swap(): return lax.ppermute(x, axis, [(0, 1), (1, 0)])  65.7 us
    pallas_call x1, Pallas kernels, backward_kept(): pl.pallas_call(functools.partial(kept_kernel, 512), grid=(FF // wide,), i...  59.4 us
    pallas_call x2, Pallas kernels, tall_gradient(): pl.pallas_call(tall_kernel, grid_spec=pltpu.PrefetchScalarGridSpec(num_sc...  53.8 us
    pallas_call x1, Pallas kernels, into(): pl.pallas_call(into_kernel, grid=(T // rows,), in_specs=[wide, wide, w, w...  52.7 us
    pallas_call x1, Pallas kernels, forward(): pl.pallas_call(functools.partial(forward_kernel, 512), grid=(FF // BN,),...  46.2 us
  transfers between devices with their start and end apart: 30, of which 4 were waited for; matrix products, arithmetic and copies ran while one was open for 0% of the time, Pallas kernels for 59%

profile of v2, /device:TPU:0, one launch (start us, length us, event | category | flops | bytes accessed | tf_op | source)
XLA Modules:
  0.0 810.3 jit_solution(7324272963169277687)
XLA Ops:
  7.2 2.6 fusion
  9.8 4.1 fusion.1.a_ref
  14.0 46.2 %forward.1 = (bf16[2048,6144]{1,0:T(8,128)(2,1)}, f32[2048,6144]{1,0:T(8,128)}) custom-call(bf16[2048,768]{1,0:T(8,128)(2,1)} %fusion.1.a_ref, bf16[2,768,6144]{2,1,0:T(8,128)(2,1)} %w_ref.6, bf16[2,768,6144]{2,1,0:T(8,128)(2,1)} %w_ref.7), custom_call_target="tpu_custom_call" | custom-call | flops 38654705664 | bytes 100000000 | tf_op jit(solution)/shard_map/forward/pallas_call | solution.py:49
  60.2 28.3 %down.1 = (bf16[2048,768]{1,0:T(8,128)(2,1)}, bf16[2048,768]{1,0:T(8,128)(2,1)}) custom-call(bf16[2048,6144]{1,0:T(8,128)(2,1)} %get-tuple-element.139.act_ref, bf16[2,6144,768]{2,1,0:T(8,128)(2,1)} %w_ref.5, bf16[2048,768]{1,0:T(8,128)(2,1)} %bitcast.7), custom_call_target="tpu_custom_call" | custom-call | flops 19327352832 | bytes 45000000 | tf_op jit(solution)/shard_map/down/pallas_call | solution.py:72
  88.4 70.5 %backward.1 = (bf16[2048,6144]{1,0:T(8,128)(2,1)}, bf16[2048,6144]{1,0:T(8,128)(2,1)}, bf16[2048,6144]{1,0:T(8,128)(2,1)}) custom-call(bf16[2048,768]{1,0:T(8,128)(2,1)} %get-tuple-element.119.a_ref, bf16[2048,768]{1,0:T(8,128)(2,1)} %bitcast.10, bf16[2,768,6144]{2,1,0:T(8,128)(2,1)} %w_ref.6, bf16[2,768,6144]{2,1,0:T(8,128)(2,1)} %w_ref.7, ...), custom_call_target="tpu_custom_call" | custom-call | flops 57982058496 | bytes 110000000 | tf_op jit(solution)/shard_map/backward/pallas_call | solution.py:106
  159.5 26.8 %tall.2 = (bf16[8,384,768]{2,1,0:T(8,128)(2,1)}, bf16[8,384,768]{2,1,0:T(8,128)(2,1)}) custom-call(s32[9]{0:T(128)} %get-tuple-element.222.where_ref, bf16[2048,6144]{1,0:T(8,128)(2,1)} %get-tuple-element.122.act_ref, bf16[2048,768]{1,0:T(8,128)(2,1)} %bitcast.11), custom_call_target="tpu_custom_call" | custom-call | flops 19327352832 | bytes 40000000 | tf_op jit(solution)/shard_map/tall/pallas_call | solution.py:232
  187.1 26.8 %wide.4 = (bf16[8,48,6144]{2,1,0:T(8,128)(2,1)}, bf16[8,48,6144]{2,1,0:T(8,128)(2,1)}) custom-call(s32[9]{0:T(128)} %get-tuple-element.222.where_ref, bf16[2048,768]{1,0:T(8,128)(2,1)} %get-tuple-element.119.a_ref, bf16[2048,6144]{1,0:T(8,128)(2,1)} %get-tuple-element.134.rhs_ref.dg_ref), custom_call_target="tpu_custom_call" | custom-call | flops 19327352832 | bytes 40000000 | tf_op jit(solution)/shard_map/wide/pallas_call | solution.py:207
  213.9 27.0 %wide.5 = (bf16[8,48,6144]{2,1,0:T(8,128)(2,1)}, bf16[8,48,6144]{2,1,0:T(8,128)(2,1)}) custom-call(s32[9]{0:T(128)} %get-tuple-element.222.where_ref, bf16[2048,768]{1,0:T(8,128)(2,1)} %get-tuple-element.119.a_ref, bf16[2048,6144]{1,0:T(8,128)(2,1)} %get-tuple-element.126.rhs_ref.du_ref), custom_call_target="tpu_custom_call" | custom-call | flops 19327352832 | bytes 40000000 | tf_op jit(solution)/shard_map/wide/pallas_call | solution.py:207
  241.4 8.2 %pair_sum.3.refs_0_ = bf16[8,48,18432]{2,1,0:T(8,128)(2,1)} custom-call(bf16[8,384,768]{2,1,0:T(8,128)(2,1)} %get-tuple-element.128.own_ref, bf16[8,384,768]{2,1,0:T(8,128)(2,1)} %collective-permute-done.got_ref), custom_call_target="tpu_custom_call" | custom-call | flops 400000000 | bytes 14155776 | tf_op jit(solution)/shard_map/pair_sum/pallas_call | solution.py:258
  249.6 8.2 %pair_sum.4.refs_0_ = bf16[8,48,18432]{2,1,0:T(8,128)(2,1)} custom-call(bf16[8,48,6144]{2,1,0:T(8,128)(2,1)} %get-tuple-element.130.own_ref, bf16[8,48,6144]{2,1,0:T(8,128)(2,1)} %collective-permute-done.1.got_ref, bf16[8,48,18432]{2,1,0:T(8,128)(2,1)} %pair_sum.3.refs_0_), custom_call_target="tpu_custom_call", output_to_operand_aliasing={{}: (2, {})} | custom-call | flops 400000000 | bytes 14155776 | tf_op jit(solution)/shard_map/pair_sum/pallas_call | solution.py:258
  257.8 8.2 %pair_sum.5 = bf16[8,48,18432]{2,1,0:T(8,128)(2,1)} custom-call(bf16[8,48,6144]{2,1,0:T(8,128)(2,1)} %get-tuple-element.132.own_ref, bf16[8,48,6144]{2,1,0:T(8,128)(2,1)} %collective-permute-done.2.got_ref, bf16[8,48,18432]{2,1,0:T(8,128)(2,1)} %pair_sum.4.refs_0_), custom_call_target="tpu_custom_call", output_to_operand_aliasing={{}: (2, {})} | custom-call | flops 400000000 | bytes 14155776 | tf_op jit(solution)/shard_map/pair_sum/pallas_call | solution.py:258
  266.1 52.7 %into.1.dy_ref = bf16[2048,768]{1,0:T(8,128)(2,1)} custom-call(bf16[2048,6144]{1,0:T(8,128)(2,1)} %get-tuple-element.134.rhs_ref.dg_ref, bf16[2048,6144]{1,0:T(8,128)(2,1)} %get-tuple-element.126.rhs_ref.du_ref, bf16[2,768,6144]{2,1,0:T(8,128)(2,1)} %w_ref.6, bf16[2,768,6144]{2,1,0:T(8,128)(2,1)} %w_ref.7, bf16[2048,768]{1,0:T(8,128)(2,1)} %get-tuple-element.118.h_ref, ...), custom_call_target="tpu_custom_call" | custom-call | flops 38654705664 | bytes 80000000 | tf_op jit(solution)/shard_map/into/pallas_call | solution.py:169
  318.8 59.4 %backward_kept.1 = (bf16[2048,6144]{1,0:T(8,128)(2,1)}, bf16[2048,6144]{1,0:T(8,128)(2,1)}) custom-call(bf16[2048,768]{1,0:T(8,128)(2,1)} %fusion.1.a_ref, bf16[2048,768]{1,0:T(8,128)(2,1)} %into.1.dy_ref, f32[2048,6144]{1,0:T(8,128)} %get-tuple-element.136.gate_ref, bf16[2,768,6144]{2,1,0:T(8,128)(2,1)} %w_ref.7, bf16[2,6144,768]{2,1,0:T(8,128)(2,1)} %w_ref.5), custom_call_target="tpu_custom_call" | custom-call | flops 38654705664 | bytes 130000000 | tf_op jit(solution)/shard_map/backward_kept/pallas_call | solution.py:139
  380.6 27.0 %tall.3 = (bf16[8,384,768]{2,1,0:T(8,128)(2,1)}, bf16[8,384,768]{2,1,0:T(8,128)(2,1)}) custom-call(s32[9]{0:T(128)} %get-tuple-element.222.where_ref, bf16[2048,6144]{1,0:T(8,128)(2,1)} %get-tuple-element.139.act_ref, bf16[2048,768]{1,0:T(8,128)(2,1)} %into.1.dy_ref), custom_call_target="tpu_custom_call" | custom-call | flops 19327352832 | bytes 40000000 | tf_op jit(solution)/shard_map/tall/pallas_call | solution.py:232
  407.6 26.8 %wide.6 = (bf16[8,48,6144]{2,1,0:T(8,128)(2,1)}, bf16[8,48,6144]{2,1,0:T(8,128)(2,1)}) custom-call(s32[9]{0:T(128)} %get-tuple-element.221.where_ref, bf16[2048,768]{1,0:T(8,128)(2,1)} %fusion.1.a_ref, bf16[2048,6144]{1,0:T(8,128)(2,1)} %get-tuple-element.141.rhs_ref), custom_call_target="tpu_custom_call" | custom-call | flops 19327352832 | bytes 40000000 | tf_op jit(solution)/shard_map/wide/pallas_call | solution.py:207
  435.0 6.4 pair_one.1
  441.4 26.8 %wide.7 = (bf16[8,48,6144]{2,1,0:T(8,128)(2,1)}, bf16[8,48,6144]{2,1,0:T(8,128)(2,1)}) custom-call(s32[9]{0:T(128)} %get-tuple-element.221.where_ref, bf16[2048,768]{1,0:T(8,128)(2,1)} %fusion.1.a_ref, bf16[2048,6144]{1,0:T(8,128)(2,1)} %get-tuple-element.145.rhs_ref), custom_call_target="tpu_custom_call" | custom-call | flops 19327352832 | bytes 40000000 | tf_op jit(solution)/shard_map/wide/pallas_call | solution.py:207
  468.2 8.8 %pair_split.2 = (f32[4,48,2048]{2,1,0:T(8,128)}, f32[4,48,2048]{2,1,0:T(8,128)}, f32[4,48,2048]{2,1,0:T(8,128)}, bf16[4,48,2048]{2,1,0:T(8,128)(2,1)}, bf16[4,48...) custom-call(bf16[8,48,6144]{2,1,0:T(8,128)(2,1)} %get-tuple-element.147.own_ref, ...), custom_call_target="tpu_custom_call" | custom-call | flops 400000000 | bytes 16515072 | tf_op jit(solution)/shard_map/pair_split/pallas_call | solution.py:310
  480.7 8.8 %pair_split.3 = (f32[4,48,2048]{2,1,0:T(8,128)}, f32[4,48,2048]{2,1,0:T(8,128)}, f32[4,48,2048]{2,1,0:T(8,128)}, bf16[4,48,2048]{2,1,0:T(8,128)(2,1)}, bf16[4,48...) custom-call(bf16[8,48,6144]{2,1,0:T(8,128)(2,1)} %get-tuple-element.150.own_ref, ...), custom_call_target="tpu_custom_call" | custom-call | flops 400000000 | bytes 16515072 | tf_op jit(solution)/shard_map/pair_split/pallas_call | solution.py:310
  489.6 20.8 %collective-permute-done.6.refs_3_ = bf16[4,48,2048]{2,1,0:T(8,128)(2,1)S(1)} collective-permute-done((bf16[4,48,2048]{2,1,0:T(8,128)(2,1)}, bf16[4,48,2048]{2,1,0:T(8,128)(2,1)S(1)}, u32[]{:S(2)}, u32[]{:S(2)}) %collective-permute-start.6) | collective-permute-done | bytes 786464 | tf_op jit(solution)/shard_map/ppermute | solution.py:405
  511.8 5.4 add_step.6
  522.6 28.2 %collective-permute-done.10.refs_4_ = bf16[4,48,2048]{2,1,0:T(8,128)(2,1)S(1)} collective-permute-done((bf16[4,48,2048]{2,1,0:T(8,128)(2,1)}, bf16[4,48,2048]{2,1,0:T(8,128)(2,1)S(1)}, u32[]{:S(2)}, u32[]{:S(2)}) %collective-permute-start.10) | collective-permute-done | bytes 786464 | tf_op jit(solution)/shard_map/ppermute | solution.py:405
  551.7 33.7 %adamw.6 = (bf16[2,6144,768]{2,1,0:T(8,128)(2,1)}, f32[2,6144,768]{2,1,0:T(8,128)}, f32[2,6144,768]{2,1,0:T(8,128)}) custom-call(bf16[2,6144,768]{2,1,0:T(8,128)(2,1)} %w_ref.5, f32[2,6144,768]{2,1,0:T(8,128)} %m_ref.9, f32[2,6144,768]{2,1,0:T(8,128)} %v_ref.9, bf16[768,18432]{1,0:T(8,128)(2,1)} %all-gather.5.cloned.1.call-done.g_ref), custom_call_target="tpu_custom_call" | custom-call | flops 19000000512 | bytes 103809024 | tf_op jit(solution)/shard_map/adamw/pallas_call | solution.py:387
  586.5 5.5 add_step.7
  593.1 3.9 add_step.8
  602.0 33.8 %adamw.7 = (bf16[2,768,6144]{2,1,0:T(8,128)(2,1)}, f32[2,768,6144]{2,1,0:T(8,128)}, f32[2,768,6144]{2,1,0:T(8,128)}) custom-call(bf16[2,768,6144]{2,1,0:T(8,128)(2,1)} %w_ref.6, f32[2,768,6144]{2,1,0:T(8,128)} %m_ref.10, f32[2,768,6144]{2,1,0:T(8,128)} %v_ref.10, bf16[768,18432]{1,0:T(8,128)(2,1)} %all-gather.5.cloned.1.call-done.g_ref), custom_call_target="tpu_custom_call" | custom-call | flops 19000000512 | bytes 103809024 | tf_op jit(solution)/shard_map/adamw/pallas_call | solution.py:387
  640.4 16.6 %collective-permute-done.18.refs_3_ = bf16[2,48,2048]{2,1,0:T(8,128)(2,1)S(1)} collective-permute-done((bf16[2,48,2048]{2,1,0:T(8,128)(2,1)S(1)}, bf16[2,48,2048]{2,1,0:T(8,128)(2,1)S(1)}, u32[]{:S(2)}, u32[]{:S(2)}) %collective-permute-start.18) | collective-permute-done | bytes 393248 | tf_op jit(solution)/shard_map/ppermute | solution.py:405
  658.1 3.9 add_step.10
  665.2 33.6 %adamw.8 = (bf16[2,768,6144]{2,1,0:T(8,128)(2,1)}, f32[2,768,6144]{2,1,0:T(8,128)}, f32[2,768,6144]{2,1,0:T(8,128)}) custom-call(bf16[2,768,6144]{2,1,0:T(8,128)(2,1)} %w_ref.7, f32[2,768,6144]{2,1,0:T(8,128)} %m_ref.11, f32[2,768,6144]{2,1,0:T(8,128)} %v_ref.11, bf16[768,18432]{1,0:T(8,128)(2,1)} %all-gather.5.cloned.1.call-done.g_ref), custom_call_target="tpu_custom_call" | custom-call | flops 19000000512 | bytes 103809024 | tf_op jit(solution)/shard_map/adamw/pallas_call | solution.py:387
  702.1 33.6 %adamw.9 = (bf16[2,6144,768]{2,1,0:T(8,128)(2,1)}, f32[2,6144,768]{2,1,0:T(8,128)}, f32[2,6144,768]{2,1,0:T(8,128)}) custom-call(bf16[2,6144,768]{2,1,0:T(8,128)(2,1)} %w_ref.5, f32[2,6144,768]{2,1,0:T(8,128)} %m_ref.9, f32[2,6144,768]{2,1,0:T(8,128)} %v_ref.9, ...), custom_call_target="tpu_custom_call", output_to_operand_aliasing={{0}: (4, {}), {1}: (5, {}), {2}: (6, {})} | custom-call | flops 19000000512 | bytes 103809024 | tf_op jit(solution)/shard_map/adamw/pallas_call | solution.py:387
  735.7 33.6 %adamw.10 = (bf16[2,768,6144]{2,1,0:T(8,128)(2,1)}, f32[2,768,6144]{2,1,0:T(8,128)}, f32[2,768,6144]{2,1,0:T(8,128)}) custom-call(bf16[2,768,6144]{2,1,0:T(8,128)(2,1)} %w_ref.6, f32[2,768,6144]{2,1,0:T(8,128)} %m_ref.10, f32[2,768,6144]{2,1,0:T(8,128)} %v_ref.10, ...), custom_call_target="tpu_custom_call", output_to_operand_aliasing={{0}: (4, {}), {1}: (5, {}), {2}: (6, {})} | custom-call | flops 19000000512 | bytes 103809024 | tf_op jit(solution)/shard_map/adamw/pallas_call | solution.py:387
  769.4 33.6 %adamw.11 = (bf16[2,768,6144]{2,1,0:T(8,128)(2,1)}, f32[2,768,6144]{2,1,0:T(8,128)}, f32[2,768,6144]{2,1,0:T(8,128)}) custom-call(bf16[2,768,6144]{2,1,0:T(8,128)(2,1)} %w_ref.7, f32[2,768,6144]{2,1,0:T(8,128)} %m_ref.11, f32[2,768,6144]{2,1,0:T(8,128)} %v_ref.11, ...), custom_call_target="tpu_custom_call", output_to_operand_aliasing={{0}: (4, {}), {1}: (5, {}), {2}: (6, {})} | custom-call | flops 19000000512 | bytes 103809024 | tf_op jit(solution)/shard_map/adamw/pallas_call | solution.py:387
  (111 shorter events, 35.3 us)
Async XLA Ops:
  7.2 373.4 %reduce-scatter.3.cloned.1.call-start = ((), (), s32[]{:S(2)}) async-start(), calls=%async_computation.2 | async-start | bytes 15925248 | tf_op jit(solution)/shard_map/reduce_scatter | solution.py:417
  186.3 55.0 %collective-permute-start = (bf16[8,384,768]{2,1,0:T(8,128)(2,1)}, bf16[8,384,768]{2,1,0:T(8,128)(2,1)}, u32[]{:S(2)}, u32[]{:S(2)}) collective-permute-start(bf16[8,384,768]{2,1,0:T(8,128)(2,1)} %get-tuple-element.129), channel_id=1, source_target_pairs={{0,1},{1,0},{2,3},{3,2},{4,5},{5,4},{6,7},{7,6},{8,9},{9,8},{10,11... | collective-permute-start | bytes 14155784 | tf_op jit(solution)/shard_map/ppermute | solution.py:405
  213.9 35.7 %collective-permute-start.1 = (bf16[8,48,6144]{2,1,0:T(8,128)(2,1)}, bf16[8,48,6144]{2,1,0:T(8,128)(2,1)}, u32[]{:S(2)}, u32[]{:S(2)}) collective-permute-start(bf16[8,48,6144]{2,1,0:T(8,128)(2,1)} %get-tuple-element.131), channel_id=1, source_target_pairs={{0,1},{1,0},{2,3},{3,2},{4,5},{5,4},{6,7},{7,6},{8,9},{9,8},{10,11... | collective-permute-start | bytes 14155784 | tf_op jit(solution)/shard_map/ppermute | solution.py:405
  240.9 16.9 %collective-permute-start.2 = (bf16[8,48,6144]{2,1,0:T(8,128)(2,1)}, bf16[8,48,6144]{2,1,0:T(8,128)(2,1)}, u32[]{:S(2)}, u32[]{:S(2)}) collective-permute-start(bf16[8,48,6144]{2,1,0:T(8,128)(2,1)} %get-tuple-element.133), channel_id=1, source_target_pairs={{0,1},{1,0},{2,3},{3,2},{4,5},{5,4},{6,7},{7,6},{8,9},{9,8},{10,11... | collective-permute-start | bytes 14155784 | tf_op jit(solution)/shard_map/ppermute | solution.py:405
  266.0 251.2 %all-gather.5.cloned.1.call-start = ((), (), s32[]{:S(2)}) async-start(), calls=%async_computation.3 | async-start | bytes 30081024 | tf_op jit(solution)/shard_map/all_gather | solution.py:413
  380.6 216.4 %reduce-scatter.5.cloned.1.call-start = ((), (), s32[]{:S(2)}) async-start(), calls=%async_computation.4 | async-start | bytes 5308416 | tf_op jit(solution)/shard_map/reduce_scatter | solution.py:417
  407.6 27.3 %collective-permute-start.3 = (bf16[8,384,768]{2,1,0:T(8,128)(2,1)}, bf16[8,384,768]{2,1,0:T(8,128)(2,1)}, u32[]{:S(2)}, u32[]{:S(2)}) collective-permute-start(bf16[8,384,768]{2,1,0:T(8,128)(2,1)} %get-tuple-element.144), channel_id=1, source_target_pairs={{0,1},{1,0},{2,3},{3,2},{4,5},{5,4},{6,7},{7,6},{8,9},{9,8},{10,11... | collective-permute-start | bytes 14155784 | tf_op jit(solution)/shard_map/ppermute | solution.py:405
  434.4 33.8 %collective-permute-start.4 = (bf16[8,48,6144]{2,1,0:T(8,128)(2,1)}, bf16[8,48,6144]{2,1,0:T(8,128)(2,1)}, u32[]{:S(2)}, u32[]{:S(2)}) collective-permute-start(bf16[8,48,6144]{2,1,0:T(8,128)(2,1)} %get-tuple-element.148), channel_id=1, source_target_pairs={{0,1},{1,0},{2,3},{3,2},{4,5},{5,4},{6,7},{7,6},{8,9},{9,8},{10,11... | collective-permute-start | bytes 14155784 | tf_op jit(solution)/shard_map/ppermute | solution.py:405
  468.2 12.5 %collective-permute-start.5 = (bf16[8,48,6144]{2,1,0:T(8,128)(2,1)}, bf16[8,48,6144]{2,1,0:T(8,128)(2,1)}, u32[]{:S(2)}, u32[]{:S(2)}) collective-permute-start(bf16[8,48,6144]{2,1,0:T(8,128)(2,1)} %get-tuple-element.151), channel_id=1, source_target_pairs={{0,1},{1,0},{2,3},{3,2},{4,5},{5,4},{6,7},{7,6},{8,9},{9,8},{10,11... | collective-permute-start | bytes 14155784 | tf_op jit(solution)/shard_map/ppermute | solution.py:405
  477.1 33.3 %collective-permute-start.6 = (bf16[4,48,2048]{2,1,0:T(8,128)(2,1)}, bf16[4,48,2048]{2,1,0:T(8,128)(2,1)S(1)}, u32[]{:S(2)}, u32[]{:S(2)}) collective-permute-start(bf16[4,48,2048]{2,1,0:T(8,128)(2,1)} %get-tuple-element.156), channel_id=1, source_target_pairs={{0,8},{8,0},{1,9},{9,1},{2,10},{10,2},{3,11},{11,3},{4,12},{12,4},... | collective-permute-start | bytes 2359304 | tf_op jit(solution)/shard_map/ppermute | solution.py:405
  478.5 31.9 %collective-permute-start.7 = (bf16[4,48,2048]{2,1,0:T(8,128)(2,1)}, bf16[4,48,2048]{2,1,0:T(8,128)(2,1)S(1)}, u32[]{:S(2)}, u32[]{:S(2)}) collective-permute-start(bf16[4,48,2048]{2,1,0:T(8,128)(2,1)} %get-tuple-element.157), channel_id=1, source_target_pairs={{0,4},{4,0},{1,5},{5,1},{2,6},{6,2},{3,7},{7,3},{8,12},{12,8},{9,1... | collective-permute-start | bytes 2359304 | tf_op jit(solution)/shard_map/ppermute | solution.py:405
  480.0 30.4 %collective-permute-start.8 = (bf16[4,48,2048]{2,1,0:T(8,128)(2,1)}, bf16[4,48,2048]{2,1,0:T(8,128)(2,1)S(1)}, u32[]{:S(2)}, u32[]{:S(2)}) collective-permute-start(bf16[4,48,2048]{2,1,0:T(8,128)(2,1)} %get-tuple-element.158), channel_id=1, source_target_pairs={{0,2},{2,0},{1,3},{3,1},{4,6},{6,4},{5,7},{7,5},{8,10},{10,8},{9,1... | collective-permute-start | bytes 2359304 | tf_op jit(solution)/shard_map/ppermute | solution.py:405
  517.3 184.8 %all-gather.7.cloned.1.call-start = ((), (), s32[]{:S(2)}) async-start(), calls=%async_computation.5 | async-start | bytes 10027008 | tf_op jit(solution)/shard_map/all_gather | solution.py:413
  517.3 33.5 %collective-permute-start.10 = (bf16[4,48,2048]{2,1,0:T(8,128)(2,1)}, bf16[4,48,2048]{2,1,0:T(8,128)(2,1)S(1)}, u32[]{:S(2)}, u32[]{:S(2)}) collective-permute-start(bf16[4,48,2048]{2,1,0:T(8,128)(2,1)} %get-tuple-element.167), channel_id=1, source_target_pairs={{0,4},{4,0},{1,5},{5,1},{2,6},{6,2},{3,7},{7,3},{8,12},{12,8},{9,1... | collective-permute-start | bytes 2359304 | tf_op jit(solution)/shard_map/ppermute | solution.py:405
  518.8 66.6 %collective-permute-start.11 = (bf16[4,48,2048]{2,1,0:T(8,128)(2,1)}, bf16[4,48,2048]{2,1,0:T(8,128)(2,1)S(1)}, u32[]{:S(2)}, u32[]{:S(2)}) collective-permute-start(bf16[4,48,2048]{2,1,0:T(8,128)(2,1)} %get-tuple-element.168), channel_id=1, source_target_pairs={{0,2},{2,0},{1,3},{3,1},{4,6},{6,4},{5,7},{7,5},{8,10},{10,8},{9,1... | collective-permute-start | bytes 2359304 | tf_op jit(solution)/shard_map/ppermute | solution.py:405
  520.3 65.1 %collective-permute-start.9 = (bf16[4,48,2048]{2,1,0:T(8,128)(2,1)}, bf16[4,48,2048]{2,1,0:T(8,128)(2,1)S(1)}, u32[]{:S(2)}, u32[]{:S(2)}) collective-permute-start(bf16[4,48,2048]{2,1,0:T(8,128)(2,1)} %get-tuple-element.166), channel_id=1, source_target_pairs={{0,8},{8,0},{1,9},{9,1},{2,10},{10,2},{3,11},{11,3},{4,12},{12,4},... | collective-permute-start | bytes 2359304 | tf_op jit(solution)/shard_map/ppermute | solution.py:405
  520.8 71.2 %collective-permute-start.12 = (bf16[2,48,2048]{2,1,0:T(8,128)(2,1)}, bf16[2,48,2048]{2,1,0:T(8,128)(2,1)S(1)}, u32[]{:S(2)}, u32[]{:S(2)}) collective-permute-start(bf16[2,48,2048]{2,1,0:T(8,128)(2,1)} %get-tuple-element.173), channel_id=1, source_target_pairs={{0,4},{4,0},{1,5},{5,1},{2,6},{6,2},{3,7},{7,3},{8,12},{12,8},{9,1... | collective-permute-start | bytes 1179656 | tf_op jit(solution)/shard_map/ppermute | solution.py:405
  522.1 70.0 %collective-permute-start.13 = (bf16[2,48,2048]{2,1,0:T(8,128)(2,1)}, bf16[2,48,2048]{2,1,0:T(8,128)(2,1)S(1)}, u32[]{:S(2)}, u32[]{:S(2)}) collective-permute-start(bf16[2,48,2048]{2,1,0:T(8,128)(2,1)} %get-tuple-element.174), channel_id=1, source_target_pairs={{0,2},{2,0},{1,3},{3,1},{4,6},{6,4},{5,7},{7,5},{8,10},{10,8},{9,1... | collective-permute-start | bytes 1179656 | tf_op jit(solution)/shard_map/ppermute | solution.py:405
  550.8 41.3 %collective-permute-start.14 = (bf16[2,48,2048]{2,1,0:T(8,128)(2,1)}, bf16[2,48,2048]{2,1,0:T(8,128)(2,1)S(1)}, u32[]{:S(2)}, u32[]{:S(2)}) collective-permute-start(bf16[2,48,2048]{2,1,0:T(8,128)(2,1)} %get-tuple-element.175), channel_id=1, source_target_pairs={{0,8},{8,0},{1,9},{9,1},{2,10},{10,2},{3,11},{11,3},{4,12},{12,4},... | collective-permute-start | bytes 1179656 | tf_op jit(solution)/shard_map/ppermute | solution.py:405
  597.0 138.7 %all-gather.9.cloned.1.call-start = ((), (), s32[]{:S(2)}) async-start(), calls=%async_computation.6 | async-start | bytes 10027008 | tf_op jit(solution)/shard_map/all_gather | solution.py:413
  597.1 38.8 %collective-permute-start.15 = (bf16[1,48,2048]{2,1,0:T(8,128)(2,1)}, bf16[1,48,2048]{2,1,0:T(8,128)(2,1)S(1)}, u32[]{:S(2)}, u32[]{:S(2)}) collective-permute-start(bf16[1,48,2048]{2,1,0:T(8,128)(2,1)} %get-tuple-element.184), channel_id=1, source_target_pairs={{0,2},{2,0},{1,3},{3,1},{4,6},{6,4},{5,7},{7,5},{8,10},{10,8},{9,1... | collective-permute-start | bytes 589832 | tf_op jit(solution)/shard_map/ppermute | solution.py:405
  598.6 37.3 %collective-permute-start.16 = (bf16[1,48,2048]{2,1,0:T(8,128)(2,1)}, bf16[1,48,2048]{2,1,0:T(8,128)(2,1)S(1)}, u32[]{:S(2)}, u32[]{:S(2)}) collective-permute-start(bf16[1,48,2048]{2,1,0:T(8,128)(2,1)} %get-tuple-element.185), channel_id=1, source_target_pairs={{0,8},{8,0},{1,9},{9,1},{2,10},{10,2},{3,11},{11,3},{4,12},{12,4},... | collective-permute-start | bytes 589832 | tf_op jit(solution)/shard_map/ppermute | solution.py:405
  599.6 39.6 %copy-start.19 = (bf16[2,48,2048]{2,1,0:T(8,128)(2,1)S(1)}, bf16[2,48,2048]{2,1,0:T(8,128)(2,1)}, u32[]{:S(2)}) copy-start(bf16[2,48,2048]{2,1,0:T(8,128)(2,1)} %get-tuple-element.191) | copy-start | bytes 1179652
  599.6 40.5 %copy-start.18 = (bf16[2,48,2048]{2,1,0:T(8,128)(2,1)S(1)}, bf16[2,48,2048]{2,1,0:T(8,128)(2,1)}, u32[]{:S(2)}) copy-start(bf16[2,48,2048]{2,1,0:T(8,128)(2,1)} %get-tuple-element.192) | copy-start | bytes 1179652
  599.6 36.3 %collective-permute-start.17 = (bf16[1,48,2048]{2,1,0:T(8,128)(2,1)}, bf16[1,48,2048]{2,1,0:T(8,128)(2,1)S(1)}, u32[]{:S(2)}, u32[]{:S(2)}) collective-permute-start(bf16[1,48,2048]{2,1,0:T(8,128)(2,1)} %get-tuple-element.186), channel_id=1, source_target_pairs={{0,4},{4,0},{1,5},{5,1},{2,6},{6,2},{3,7},{7,3},{8,12},{12,8},{9,1... | collective-permute-start | bytes 589832 | tf_op jit(solution)/shard_map/ppermute | solution.py:405
  639.0 130.3 %all-gather.11.cloned.1.call-start = ((), (), s32[]{:S(2)}) async-start(), calls=%async_computation.7 | async-start | bytes 10027008 | tf_op jit(solution)/shard_map/all_gather | solution.py:413
  639.1 17.9 %collective-permute-start.18 = (bf16[2,48,2048]{2,1,0:T(8,128)(2,1)S(1)}, bf16[2,48,2048]{2,1,0:T(8,128)(2,1)S(1)}, u32[]{:S(2)}, u32[]{:S(2)}) collective-permute-start(bf16[2,48,2048]{2,1,0:T(8,128)(2,1)S(1)} %copy-done.20), channel_id=1, source_target_pairs={{0,4},{4,0},{1,5},{5,1},{2,6},{6,2},{3,7},{7,3},{8,12},{12,8},{9,1... | collective-permute-start | bytes 1179656 | tf_op jit(solution)/shard_map/ppermute | solution.py:405
  639.3 17.8 %collective-permute-start.19 = (bf16[2,48,2048]{2,1,0:T(8,128)(2,1)S(1)}, bf16[2,48,2048]{2,1,0:T(8,128)(2,1)S(1)}, u32[]{:S(2)}, u32[]{:S(2)}) collective-permute-start(bf16[2,48,2048]{2,1,0:T(8,128)(2,1)S(1)} %copy-done.19), channel_id=1, source_target_pairs={{0,2},{2,0},{1,3},{3,1},{4,6},{6,4},{5,7},{7,5},{8,10},{10,8},{9,1... | collective-permute-start | bytes 1179656 | tf_op jit(solution)/shard_map/ppermute | solution.py:405
  640.1 16.9 %collective-permute-start.20 = (bf16[2,48,2048]{2,1,0:T(8,128)(2,1)S(1)}, bf16[2,48,2048]{2,1,0:T(8,128)(2,1)S(1)}, u32[]{:S(2)}, u32[]{:S(2)}) collective-permute-start(bf16[2,48,2048]{2,1,0:T(8,128)(2,1)S(1)} %copy-done.18), channel_id=1, source_target_pairs={{0,8},{8,0},{1,9},{9,1},{2,10},{10,2},{3,11},{11,3},{4,12},{12,4},... | collective-permute-start | bytes 1179656 | tf_op jit(solution)/shard_map/ppermute | solution.py:405
  662.0 36.9 %collective-permute-start.21 = (bf16[1,48,2048]{2,1,0:T(8,128)(2,1)}, bf16[1,48,2048]{2,1,0:T(8,128)(2,1)S(1)}, u32[]{:S(2)}, u32[]{:S(2)}) collective-permute-start(bf16[1,48,2048]{2,1,0:T(8,128)(2,1)} %get-tuple-element.199), channel_id=1, source_target_pairs={{0,2},{2,0},{1,3},{3,1},{4,6},{6,4},{5,7},{7,5},{8,10},{10,8},{9,1... | collective-permute-start | bytes 589832 | tf_op jit(solution)/shard_map/ppermute | solution.py:405
  663.2 35.7 %collective-permute-start.22 = (bf16[1,48,2048]{2,1,0:T(8,128)(2,1)}, bf16[1,48,2048]{2,1,0:T(8,128)(2,1)S(1)}, u32[]{:S(2)}, u32[]{:S(2)}) collective-permute-start(bf16[1,48,2048]{2,1,0:T(8,128)(2,1)} %get-tuple-element.200), channel_id=1, source_target_pairs={{0,8},{8,0},{1,9},{9,1},{2,10},{10,2},{3,11},{11,3},{4,12},{12,4},... | collective-permute-start | bytes 589832 | tf_op jit(solution)/shard_map/ppermute | solution.py:405
  663.7 35.1 %collective-permute-start.23 = (bf16[1,48,2048]{2,1,0:T(8,128)(2,1)}, bf16[1,48,2048]{2,1,0:T(8,128)(2,1)S(1)}, u32[]{:S(2)}, u32[]{:S(2)}) collective-permute-start(bf16[1,48,2048]{2,1,0:T(8,128)(2,1)} %get-tuple-element.201), channel_id=1, source_target_pairs={{0,4},{4,0},{1,5},{5,1},{2,6},{6,2},{3,7},{7,3},{8,12},{12,8},{9,1... | collective-permute-start | bytes 589832 | tf_op jit(solution)/shard_map/ppermute | solution.py:405
  (19 other events, 88.9 us)
Sparse Core Ops, SparseCore 0:
  266.1 114.3 reduce-scatter.2
  382.8 126.9 all-gather.4
  517.4 68.7 reduce-scatter.4
  597.2 61.7 all-gather.6
  661.0 52.1 all-gather.8
  715.3 52.0 all-gather.10
